TPU v7x, 32 devices: a whole 2x2x4 slice. The times are simulated.
32 devices in a mesh: batch: 8 (over y, x, core), heads: 4 (over z).
Axes of the slice: x: 2, y: 2, z: 4, core: 2. Of those that a mesh axis runs over, the one named last changes fastest.
Arguments:
- tokens: bfloat16 [24576, 768], P('batch'), may hold values from -5 to 5
- qkv_weight: bfloat16 [768, 3, 768], P(None, None, 'heads'), may hold values from -0.21875 to 0.21875
- qv_bias: float32 [2, 768], replicated, may hold values from -3 to 3
- conv_weight: float32 [12, 33], replicated, may hold values from -0.875 to 0.875
- out_weight: bfloat16 [768, 768], P('heads'), may hold values from -0.21875 to 0.21875
- out_bias: float32 [768], replicated, may hold values from -1.75 to 1.75
- norm1_gain: float32 [768], replicated, may hold values from 0.5 to 1.5
- norm1_bias: float32 [768], replicated, may hold values from -1.75 to 1.75
- ffn_in_weight: bfloat16 [768, 3072], P(None, ('batch', 'heads')), may hold values from -0.21875 to 0.21875
- ffn_in_bias: bfloat16 [3072], P(('batch', 'heads')), may hold values from -3 to 3
- ffn_out_weight: bfloat16 [3072, 768], P(('batch', 'heads')), may hold values from -0.109375 to 0.109375
- ffn_out_bias: float32 [768], replicated, may hold values from -1.75 to 1.75
- norm2_gain: float32 [768], replicated, may hold values from 0.5 to 1.5
- norm2_bias: float32 [768], replicated, may hold values from -1.75 to 1.75
- cotangent: bfloat16 [24576, 768], P(('batch', 'heads')), may hold values from -12 to 12
- seq_lengths: int32 [24], P('batch'), may hold values from 0 to 3072, as said below
- segment_ids: int32 [24576], P('batch'), may hold values from 0 to 3, as said below
- landmark_bounds: int32 [24, 64], P('batch'), may hold values from 0 to 3024, as said below
Outputs:
- out: bfloat16 [24576, 768], P(('batch', 'heads'))
- input_grad: float32 [24576, 768], P(('batch', 'heads'))
- qkv_weight_grad: float32 [768, 3, 768], P('batch', None, 'heads')
- qv_bias_grad: float32 [2, 768], P(None, 'heads')
- conv_grad: float32 [12, 33], P('heads')
- out_weight_grad: float32 [768, 768], P('heads', 'batch')
- ffn_in_grad: float32 [768, 3072], P(None, ('batch', 'heads'))
- ffn_in_bias_grad: float32 [3072], P(('batch', 'heads'))
- ffn_out_grad: float32 [3072, 768], P(('batch', 'heads'))
- vector_grads: float32 [6, 768], P(None, ('batch', 'heads'))
- condition: float32 [], replicated
Inputs may be any that keep to these rules, and one draw needn't show every extreme that they name: `seq_lengths`: each index of batch holds 3 slots: sequences of 1024 to 3072 tokens first, then empty slots of length 0; the lengths of one index sum to at most 3072; at least one index holds a single sequence of 3072 tokens. `segment_ids`: the live tokens of an index of batch lie in order of slot from its first token slot on, each slot's tokens contiguous; the remaining token slots carry 3. landmark_bounds[s, j] = (j times the length of slot s) // 64.
All inputs are finite; a program needn't handle non-finite values.
Results may differ from a plain program's by a relative error of at most 0.013.
Values may be sent and summed in bfloat16 or wider, within the bound.
A program may use at most 448 MiB of HBM per device.

v0:
```python
from functools import partial

import jax
import jax.numpy as jnp
from jax import lax
from jax.sharding import PartitionSpec as P

HEAD_DIM = 64
PINV_ITERS = 6


best_precision = lax.Precision.HIGHEST
mask_fill = -1000000000.0
norm_eps = 1e-05
contract_rows = (((0,), (0,)), ((), ()))
contract_cols = (((1,), (1,)), ((), ()))


def split_up(x, dim, peers):
    before, after = (x.shape[:dim], x.shape[dim + 1 :])
    return jnp.moveaxis(x.reshape(*before, peers, -1, *after), dim, 0)


def sum_at_owner(x, axis, dim):
    peers = lax.axis_size(axis)
    tiles = lax.all_to_all(split_up(x, dim, peers), axis, 0, 0, tiled=True)
    return jnp.sum(tiles.astype(jnp.float32), axis=0)


def layer_norm(row_data, gain_vec, shift_vec):
    centre = row_data - jnp.mean(row_data, axis=1, keepdims=True)
    spread = jnp.mean(centre * centre, axis=1, keepdims=True)
    return centre * lax.rsqrt(spread + norm_eps) * gain_vec[None, :] + shift_vec[None, :]


def gelu_exact(values):
    return jax.nn.gelu(values, approximate=False)


def pack_layout(lengths, slot_ids, bounds):
    slot_count = lengths.shape[0]
    tok_count = slot_ids.shape[0]
    mark_count = bounds.shape[1]
    starts = jnp.cumsum(lengths) - lengths
    slot_hit = slot_ids[:, None] == jnp.arange(slot_count, dtype=jnp.int32)[None, :]
    tok_start = jnp.sum(jnp.where(slot_hit, starts[None, :], 0), axis=1)
    position = jnp.arange(tok_count, dtype=jnp.int32) - tok_start
    tok_bounds = jnp.sum(jnp.where(slot_hit[:, :, None], bounds[None, :, :], 0), axis=1)
    mark_index = jnp.sum((tok_bounds <= position[:, None]).astype(jnp.int32), axis=1) - 1
    mark_id = slot_ids * mark_count + mark_index
    all_marks = slot_count * mark_count
    member = (jnp.arange(all_marks, dtype=jnp.int32)[:, None] == mark_id[None, :]).astype(
        jnp.float32
    )
    inv_count = 1.0 / jnp.maximum(jnp.sum(member, axis=1), 1.0)
    same_slot = slot_ids[:, None] == (jnp.arange(all_marks, dtype=jnp.int32) // mark_count)[None, :]
    live_tok = (slot_ids < slot_count).astype(jnp.float32)
    live_slot = (lengths > 0).astype(jnp.float32)
    return (member, inv_count, same_slot, slot_ids, live_tok, live_slot)


def batch_mul(left, right):
    return jnp.einsum("...ij,...jk->...ik", left, right, precision=best_precision)


def newton_inverse(middle_kernel):
    mark_count = middle_kernel.shape[-1]
    column_sums = jnp.sum(middle_kernel, axis=-2)
    col_bound = jnp.max(column_sums, axis=-1)
    inverse = jnp.swapaxes(middle_kernel, -1, -2) / col_bound[..., None, None]
    identity_mat = jnp.eye(mark_count, dtype=jnp.float32)
    for sweep_index in range(PINV_ITERS):
        product = batch_mul(middle_kernel, inverse)
        inner_poly = 7.0 * identity_mat - product
        inner_poly = 15.0 * identity_mat - batch_mul(product, inner_poly)
        inner_poly = 13.0 * identity_mat - batch_mul(product, inner_poly)
        inverse = 0.25 * batch_mul(inverse, inner_poly)
    return (inverse, col_bound)


def head_mix(q_rows, k_rows, v_rows, conv_taps, layout):
    member, inv_count, same_slot, token_slot, live_tok, live_slot = layout
    slot_count = live_slot.shape[0]
    tok_count, head_dim = q_rows.shape
    mark_count = member.shape[0] // slot_count
    root_scale = head_dim ** (-0.25)
    q_scaled = q_rows * root_scale
    k_scaled = k_rows * root_scale
    q_marks = jnp.dot(member, q_scaled, precision=best_precision) * inv_count[:, None]
    k_marks = jnp.dot(member, k_scaled, precision=best_precision) * inv_count[:, None]
    first_scores = jnp.where(
        same_slot, jnp.dot(q_scaled, k_marks.T, precision=best_precision), mask_fill
    )
    first_kernel = jax.nn.softmax(first_scores, axis=1)
    q_blocks = q_marks.reshape(slot_count, mark_count, head_dim)
    k_blocks = k_marks.reshape(slot_count, mark_count, head_dim)
    middle_kernel = jax.nn.softmax(
        jnp.einsum("sid,sjd->sij", q_blocks, k_blocks, precision=best_precision), axis=2
    )
    inverse, col_bound = newton_inverse(middle_kernel)
    last_scores = jnp.where(
        same_slot.T, jnp.dot(q_marks, k_scaled.T, precision=best_precision), mask_fill
    )
    last_kernel = jax.nn.softmax(last_scores, axis=1)
    mark_values = jnp.dot(last_kernel, v_rows, precision=best_precision)
    mixed_marks = jnp.einsum(
        "sij,sjd->sid",
        inverse,
        mark_values.reshape(slot_count, mark_count, head_dim),
        precision=best_precision,
    ).reshape(slot_count * mark_count, head_dim)
    attended = jnp.dot(first_kernel, mixed_marks, precision=best_precision)
    half_width = conv_taps.shape[0] // 2
    padded_v = jnp.pad(v_rows, ((half_width, half_width), (0, 0)))
    padded_slot = jnp.pad(token_slot, (half_width, half_width), constant_values=-1)
    convolved = jnp.zeros_like(v_rows)
    for tap_index in range(conv_taps.shape[0]):
        same_seq = (padded_slot[tap_index : tap_index + tok_count] == token_slot).astype(
            jnp.float32
        )
        convolved = (
            convolved
            + conv_taps[tap_index] * padded_v[tap_index : tap_index + tok_count] * same_seq[:, None]
        )
    mixed_rows = (attended + convolved) * live_tok[:, None]
    return (mixed_rows, jnp.sum(col_bound * live_slot))


def heads_mix(layout, q_all, k_all, v_all, conv_all):
    tok_count = q_all.shape[0]
    head_count = conv_all.shape[0]
    head_dim = q_all.shape[1] // head_count

    def split_heads(row_data):
        return jnp.transpose(row_data.reshape(tok_count, head_count, head_dim), (1, 0, 2))

    def one_head(operands):
        return head_mix(operands[0], operands[1], operands[2], operands[3], layout)

    mixed_rows, bound_sums = lax.map(
        jax.checkpoint(one_head),
        (split_heads(q_all), split_heads(k_all), split_heads(v_all), conv_all),
    )
    merged = jnp.transpose(mixed_rows, (1, 0, 2)).reshape(tok_count, head_count * head_dim)
    return (merged, jnp.sum(bound_sums))


def body(
    tokens,
    qkv_weight,
    qv_bias,
    conv_weight,
    out_weight,
    out_bias,
    norm1_gain,
    norm1_bias,
    ffn_in_weight,
    ffn_in_bias,
    ffn_out_weight,
    ffn_out_bias,
    norm2_gain,
    norm2_bias,
    cotangent,
    seq_lengths,
    segment_ids,
    landmark_bounds,
):
    tok_count, model_width = tokens.shape
    head_width = qkv_weight.shape[2]
    heads_here = head_width // HEAD_DIM
    head_total = conv_weight.shape[0]
    kernel_taps = conv_weight.shape[1]
    quarter = tok_count // lax.axis_size("heads")
    head_index = lax.axis_index("heads")
    own_start = head_index * quarter
    layout = pack_layout(seq_lengths, segment_ids, landmark_bounds)
    own_rows_low = lax.dynamic_slice_in_dim(tokens, own_start, quarter, 0)
    own_tokens = own_rows_low.astype(jnp.float32)
    conv_own = lax.dynamic_slice_in_dim(conv_weight, head_index * heads_here, heads_here, 0)
    qv_own = lax.dynamic_slice_in_dim(qv_bias, head_index * head_width, head_width, 1)
    flat_qkv = qkv_weight.reshape(model_width, 3 * head_width)
    projected = jnp.dot(tokens, flat_qkv, preferred_element_type=jnp.float32).reshape(
        tok_count, 3, head_width
    )
    bias_rows = jnp.stack([qv_own[0], jnp.zeros_like(qv_own[0]), qv_own[1]])
    qkv_low = (projected + bias_rows[None, :, :]).astype(jnp.bfloat16)
    qkv_wide = lax.optimization_barrier(qkv_low).astype(jnp.float32)
    (mixed_rows, bound_total), mix_pull = jax.vjp(
        partial(heads_mix, layout), qkv_wide[:, 0], qkv_wide[:, 1], qkv_wide[:, 2], conv_own
    )
    mixed_low = mixed_rows.astype(jnp.bfloat16)
    row_block = mixed_low
    attn_part = lax.psum_scatter(
        jnp.dot(row_block, out_weight, preferred_element_type=jnp.float32).astype(jnp.bfloat16),
        "heads",
        scatter_dimension=0,
        tiled=True,
    ).astype(jnp.float32)
    live_count = jnp.sum(layout[5]) * heads_here
    first_res = own_tokens + attn_part + out_bias[None, :]
    norm1_out, norm1_pull = jax.vjp(layer_norm, first_res, norm1_gain, norm1_bias)
    norm1_low = norm1_out.astype(jnp.bfloat16)
    whole_in, whole_in_bias, whole_out = (
        lax.all_gather(ffn_in_weight, ("batch", "heads"), axis=1, tiled=True),
        lax.all_gather(ffn_in_bias, ("batch", "heads"), axis=0, tiled=True),
        lax.all_gather(ffn_out_weight, ("batch", "heads"), axis=0, tiled=True),
    )
    pre_act = (
        jnp.dot(norm1_low, whole_in, preferred_element_type=jnp.float32)
        + whole_in_bias.astype(jnp.float32)[None, :]
    )
    hidden_act, gelu_pull = jax.vjp(gelu_exact, pre_act)
    hidden_low = hidden_act.astype(jnp.bfloat16)
    ffn_result = (
        jnp.dot(hidden_low, whole_out, preferred_element_type=jnp.float32) + ffn_out_bias[None, :]
    )
    final_out, norm2_pull = jax.vjp(layer_norm, norm1_out + ffn_result, norm2_gain, norm2_bias)
    grad_second, grad_gain_two, grad_shift_two = norm2_pull(cotangent.astype(jnp.float32))
    grad_ffn_low = grad_second.astype(jnp.bfloat16)
    grad_ffn_bias = jnp.sum(grad_ffn_low.astype(jnp.float32), axis=0)
    down_term = lax.dot_general(
        hidden_low, grad_ffn_low, contract_rows, preferred_element_type=jnp.float32
    )
    grad_hidden = lax.dot_general(
        grad_ffn_low, whole_out, contract_cols, preferred_element_type=jnp.float32
    )
    grad_pre = gelu_pull(grad_hidden)[0].astype(jnp.bfloat16)
    grad_in_bias = jnp.sum(grad_pre.astype(jnp.float32), axis=0)
    up_term = lax.dot_general(
        norm1_low, grad_pre, contract_rows, preferred_element_type=jnp.float32
    )
    grad_norm1 = grad_second + lax.dot_general(
        grad_pre, whole_in, contract_cols, preferred_element_type=jnp.float32
    )
    grad_first, grad_gain_one, grad_shift_one = norm1_pull(grad_norm1)
    grad_attn_low = grad_first.astype(jnp.bfloat16)
    grad_out_bias = jnp.sum(grad_attn_low.astype(jnp.float32), axis=0)
    piece_rows = lax.all_gather(grad_attn_low, "heads", axis=0, tiled=True)
    local_grad = lax.dot_general(
        piece_rows, out_weight, contract_cols, preferred_element_type=jnp.float32
    )
    grad_mix = local_grad
    grad_weight = lax.dot_general(
        mixed_low, piece_rows, contract_rows, preferred_element_type=jnp.float32
    )
    grad_mix, out_part = (grad_mix, grad_weight)
    grad_mix_low = lax.optimization_barrier(grad_mix.astype(jnp.bfloat16)).astype(jnp.float32)
    grad_query, grad_key, grad_value, grad_conv = mix_pull(
        (grad_mix_low, jnp.zeros((), jnp.float32))
    )
    grad_qkv = jnp.stack([grad_query, grad_key, grad_value], axis=1).astype(jnp.bfloat16)
    grad_qv_own = jnp.stack(
        [
            jnp.sum(grad_qkv[:, 0].astype(jnp.float32), axis=0),
            jnp.sum(grad_qkv[:, 2].astype(jnp.float32), axis=0),
        ]
    )
    flat_grad = grad_qkv.reshape(tok_count, 3 * head_width)
    qkv_part = lax.dot_general(
        tokens, flat_grad, contract_rows, preferred_element_type=jnp.float32
    ).reshape(model_width, 3, head_width)
    row_block = flat_grad
    input_part = lax.psum_scatter(
        lax.dot_general(
            row_block, flat_qkv, contract_cols, preferred_element_type=jnp.float32
        ).astype(jnp.bfloat16),
        "heads",
        scatter_dimension=0,
        tiled=True,
    ).astype(jnp.float32)
    input_grad = grad_first + input_part
    conv_full = lax.dynamic_update_slice_in_dim(
        jnp.zeros((head_total, kernel_taps), jnp.float32), grad_conv, head_index * heads_here, 0
    )
    bias_full = lax.dynamic_update_slice_in_dim(
        jnp.zeros((2, head_total * HEAD_DIM), jnp.float32), grad_qv_own, head_index * head_width, 1
    )
    qkv_share, out_share = (
        sum_at_owner(qkv_part.astype(jnp.bfloat16), "batch", 0),
        sum_at_owner(out_part.astype(jnp.bfloat16), "batch", 1),
    )
    vector_all = jnp.stack(
        [grad_ffn_bias, grad_gain_two, grad_shift_two, grad_gain_one, grad_shift_one, grad_out_bias]
    )
    up_share, in_bias_share, down_share, vector_share = (
        lax.psum_scatter(up_term, ("batch", "heads"), scatter_dimension=1, tiled=True),
        lax.psum_scatter(grad_in_bias, ("batch", "heads"), scatter_dimension=0, tiled=True),
        lax.psum_scatter(down_term, ("batch", "heads"), scatter_dimension=0, tiled=True),
        lax.psum_scatter(vector_all, ("batch", "heads"), scatter_dimension=1, tiled=True),
    )
    conv_sum, bias_sum, bound_all, count_all = lax.psum(
        (conv_full, bias_full, bound_total, live_count), ("batch", "heads")
    )
    conv_out = lax.dynamic_slice_in_dim(conv_sum, head_index * heads_here, heads_here, 0)
    bias_out = lax.dynamic_slice_in_dim(bias_sum, head_index * head_width, head_width, 1)
    condition = bound_all / count_all
    return (
        final_out.astype(jnp.bfloat16),
        input_grad,
        qkv_share,
        bias_out,
        conv_out,
        out_share,
        up_share,
        in_bias_share,
        down_share,
        vector_share,
        condition,
    )


def solution(mesh):
    in_specs = (
        P("batch", None),
        P(None, None, "heads"),
        P(),
        P(),
        P("heads", None),
        P(),
        P(),
        P(),
        P(None, ("batch", "heads")),
        P(("batch", "heads")),
        P(("batch", "heads"), None),
        P(),
        P(),
        P(),
        P(("batch", "heads"), None),
        P("batch"),
        P("batch"),
        P("batch", None),
    )
    out_specs = (
        P(("batch", "heads"), None),
        P(("batch", "heads"), None),
        P("batch", None, "heads"),
        P(None, "heads"),
        P("heads", None),
        P("heads", "batch"),
        P(None, ("batch", "heads")),
        P(("batch", "heads")),
        P(("batch", "heads"), None),
        P(None, ("batch", "heads")),
        P(),
    )
    return jax.shard_map(body, mesh=mesh, in_specs=in_specs, out_specs=out_specs, check_vma=False)
```

profile of v0, /device:TPU:0, one launch (start us, length us, event | category | flops | bytes accessed | tf_op | source)
XLA Modules:
  0.0 1467.2 jit_solution(8246713149489868916)
XLA Ops:
  40.1 224.6 %while.41 = (s32[]{:T(128)}, bf16[3,3072,64]{1,2,0:T(8,128)(2,1)}, f32[3]{0:T(128)}, f32[3,3072,64]{2,1,0:T(8,128)}, f32[3,3072,64]{2,1,0:T(8,128)}, /*index=5*/...) while((s32[]{:T(128)}, bf16[3,3072,64]{1,2,0:T(8,128)(2,1)}, ...), condition=%wide.region_15.16_spmd.clone.clone.clone, body=%wide.region_5.15_spmd.clone.clone.clone.sunk | while | flops 2994648576 | bytes 44281500 | solution.py:140
  93.0 30.5 %fusion.1216 = bf16[3,3072,64]{1,2,0:T(8,128)(2,1)S(1)} fusion(bf16[3,3072,64]{1,2,0:T(8,128)(2,1)S(1)} %copy-done.43, s32[]{:T(128)S(6)} %copy.285, f32[192,64]{1,0:T(8,128)S(1)} %bitcast.1284, f32[3072,192]{0,1:T(8,128)S(1)} %get-tuple-element.2748, f32[3072]{0:T(1024)S(1)} %fusion.1213, f32[3072]{0:T(1024)S(1)} %get-tuple-element.2749, ...), kind=kOutput, calls=%fused_computation.368.clone.1 | convolution fusion | flops 473628672 | bytes 4460680 | tf_op jit(solution)/shard_map/jvp()/while/body/eval_jaxpr/dot_general | solution.py:112
  162.9 30.5 %fusion.1216 = bf16[3,3072,64]{1,2,0:T(8,128)(2,1)S(1)} fusion(bf16[3,3072,64]{1,2,0:T(8,128)(2,1)S(1)} %copy-done.43, s32[]{:T(128)S(6)} %copy.285, f32[192,64]{1,0:T(8,128)S(1)} %bitcast.1284, f32[3072,192]{0,1:T(8,128)S(1)} %get-tuple-element.2748, f32[3072]{0:T(1024)S(1)} %fusion.1213, f32[3072]{0:T(1024)S(1)} %get-tuple-element.2749, ...), kind=kOutput, calls=%fused_computation.368.clone.1 | convolution fusion | flops 473628672 | bytes 4460680 | tf_op jit(solution)/shard_map/jvp()/while/body/eval_jaxpr/dot_general | solution.py:112
  232.8 30.5 %fusion.1216 = bf16[3,3072,64]{1,2,0:T(8,128)(2,1)S(1)} fusion(bf16[3,3072,64]{1,2,0:T(8,128)(2,1)S(1)} %copy-done.43, s32[]{:T(128)S(6)} %copy.285, f32[192,64]{1,0:T(8,128)S(1)} %bitcast.1284, f32[3072,192]{0,1:T(8,128)S(1)} %get-tuple-element.2748, f32[3072]{0:T(1024)S(1)} %fusion.1213, f32[3072]{0:T(1024)S(1)} %get-tuple-element.2749, ...), kind=kOutput, calls=%fused_computation.368.clone.1 | convolution fusion | flops 473628672 | bytes 4460680 | tf_op jit(solution)/shard_map/jvp()/while/body/eval_jaxpr/dot_general | solution.py:112
  271.2 46.9 %all-reduce.70 = bf16[3072]{0:T(1024)(128)(2,1)S(1)} all-reduce(bf16[3072]{0:T(1024)(128)(2,1)S(1)} %dynamic-update-slice), channel_id=1, replica_groups=mesh['batch'=8,'heads'=4] {'batch','heads'}, use_global_device_ids=true, to_apply=%add.70 | all-reduce | flops 3072 | bytes 12288
  318.1 43.3 %reduce-scatter.6.cloned.1.call-done = bf16[768,768]{1,0:T(8,128)(2,1)} async-done(((bf16[3072,768]{1,0:T(8,128)(2,1)}), bf16[768,768]{1,0:T(8,128)(2,1)}) %reduce-scatter.6.cloned.1.call-update) | async-done | bytes 1179664 | tf_op jit(solution)/shard_map/reduce_scatter | solution.py:193
  365.7 39.4 %all-gather.4.cloned.1.call-done = bf16[768,3072]{0,1:T(8,128)(2,1)} async-done(((bf16[768,96]{0,1:T(8,128)(2,1)}), bf16[768,3072]{0,1:T(8,128)(2,1)}) %all-gather.4.cloned.1.call-update) | async-done | bytes 4718608 | tf_op jit(solution)/shard_map/all_gather | solution.py:204
  405.1 30.0 %multiply_convert_fusion = (bf16[768,3072]{1,0:T(8,128)(2,1)}, f32[768,3072]{1,0:T(8,128)}, f32[768,3072]{1,0:T(8,128)}) fusion(f32[3072]{0:T(1024)S(1)} %convert_element_type.470, bf16[768,3072]{0,1:T(8,128)(2,1)} %all-gather.4.cloned.1.call-done, f32[768]{0:T(1024)S(1)} %copy-done.130, f32[768]{0:T(1024)S(1)} %copy-done.121, f32[768]{0:T(1024)S(1)} %fusion.363, ...), kind=kOutput, calls=%fused_computation.512 | convolution fusion | flops 3784900608 | bytes 30698500 | tf_op jit(solution)/shard_map/dot_general | solution.py:209
  435.1 34.5 %all-gather.6.cloned.1.call-done = bf16[3072,768]{1,0:T(8,128)(2,1)} async-done(((bf16[96,768]{1,0:T(8,128)(2,1)}), bf16[3072,768]{1,0:T(8,128)(2,1)}) %all-gather.6.cloned.1.call-update) | async-done | bytes 4718608 | tf_op jit(solution)/shard_map/all_gather | solution.py:206
  469.6 8.6 fusion.386
  483.9 13.4 convert_reduce_fusion.1
  497.3 8.4 multiply_reduce_fusion.37
  510.4 87.9 %all-gather.8.cloned.1.call-done = bf16[3072,768]{1,0:T(8,128)(2,1)} async-done(((bf16[768,768]{1,0:T(8,128)(2,1)}), bf16[3072,768]{1,0:T(8,128)(2,1)}) %all-gather.8.cloned.1.call-update) | async-done | bytes 4718608 | tf_op jit(solution)/shard_map/all_gather | solution.py:238
  608.1 471.6 %while.40 = (s32[]{:T(128)}, bf16[3,3072,64]{1,2,0:T(8,128)(2,1)}, bf16[3,3072,64]{1,2,0:T(8,128)(2,1)}, bf16[3,3072,64]{1,2,0:T(8,128)(2,1)}, f32[3,33]{1,0:T(4...) while((s32[]{:T(128)}, bf16[3,3072,64]{1,2,0:T(8,128)(2,1)}, ...), condition=%wide.region_72.73_spmd.clone.clone, body=%wide.region_25.72_spmd.clone.clone.sunk | while | flops 7593409024 | bytes 344024704 | solution.py:140
  709.8 7.9 multiply_reduce_fusion.55
  717.6 20.7 %add_bitcast_fusion.2 = f32[1,33]{1,0:T(1,128)S(1)} fusion(f32[1]{0:T(128)} %bitcast.1088, f32[1]{0:T(128)} %bitcast.1089, f32[1]{0:T(128)} %bitcast.1090, f32[1]{0:T(128)} %bitcast.1091, f32[1]{0:T(128)} %bitcast.1092, f32[1]{0:T(128)} %bitcast.1093, f32[1]{0:T(128)} %bitcast.1094, f32[1]{0:T(128)} %bitcast.1095, f32[1]{0:T(128)} %bitcast.1096, ...), kind=kLoop, calls=%fused_computation.342.clone.1 | loop fusion | flops 1056 | bytes 264 | tf_op jit(solution)/shard_map/transpose(jvp())/while/body/jit(dynamic_update_index_in_dim)/broadcast_in_dim | solution.py:140
  872.2 20.8 %add_bitcast_fusion.2 = f32[1,33]{1,0:T(1,128)S(1)} fusion(f32[1]{0:T(128)} %bitcast.1088, f32[1]{0:T(128)} %bitcast.1089, f32[1]{0:T(128)} %bitcast.1090, f32[1]{0:T(128)} %bitcast.1091, f32[1]{0:T(128)} %bitcast.1092, f32[1]{0:T(128)} %bitcast.1093, f32[1]{0:T(128)} %bitcast.1094, f32[1]{0:T(128)} %bitcast.1095, f32[1]{0:T(128)} %bitcast.1096, ...), kind=kLoop, calls=%fused_computation.342.clone.1 | loop fusion | flops 1056 | bytes 264 | tf_op jit(solution)/shard_map/transpose(jvp())/while/body/jit(dynamic_update_index_in_dim)/broadcast_in_dim | solution.py:140
  1019.1 7.9 multiply_reduce_fusion.55
  1026.9 20.7 %add_bitcast_fusion.2 = f32[1,33]{1,0:T(1,128)S(1)} fusion(f32[1]{0:T(128)} %bitcast.1088, f32[1]{0:T(128)} %bitcast.1089, f32[1]{0:T(128)} %bitcast.1090, f32[1]{0:T(128)} %bitcast.1091, f32[1]{0:T(128)} %bitcast.1092, f32[1]{0:T(128)} %bitcast.1093, f32[1]{0:T(128)} %bitcast.1094, f32[1]{0:T(128)} %bitcast.1095, f32[1]{0:T(128)} %bitcast.1096, ...), kind=kLoop, calls=%fused_computation.342.clone.1 | loop fusion | flops 1056 | bytes 264 | tf_op jit(solution)/shard_map/transpose(jvp())/while/body/jit(dynamic_update_index_in_dim)/broadcast_in_dim | solution.py:140
  1090.6 10.5 fusion.366
  1102.4 8.7 fusion.407
  1141.5 49.4 %all-reduce.73 = (f32[2,768]{1,0:T(2,128)S(1)}, f32[12,33]{1,0:T(8,128)S(1)}, f32[3072]{0:T(1024)S(1)}, f32[6,768]{1,0:T(8,128)S(1)}, f32[]{:T(128)}, /*index=5*/f32[]{:T(128)}) all-reduce(f32[2,768]{1,0:T(2,128)S(1)} %dynamic_update_slice.61, ...), channel_id=1, replica_groups=mesh['batch'=8,'heads'=4] {'batch','heads'}, use_global_device_ids=true, to_apply=%region_77.78 | all-reduce | flops 9614 | bytes 76912 | tf_op jit(solution)/shard_map/psum | solution.py:291
  1202.0 115.1 %reduce-scatter.10.cloned.1.call-done = f32[768,96]{0,1:T(8,128)} async-done(((f32[768,3072]{0,1:T(8,128)}), f32[768,96]{0,1:T(8,128)}) %reduce-scatter.10.cloned.1.call-update) | async-done | bytes 294928 | tf_op jit(solution)/shard_map/reduce_scatter | solution.py:286
  1317.0 141.7 %reduce-scatter.12.cloned.1.call-done = f32[96,768]{1,0:T(8,128)} async-done(((f32[3072,768]{1,0:T(8,128)}), f32[96,768]{1,0:T(8,128)}) %reduce-scatter.12.cloned.1.call-update) | async-done | bytes 294928 | tf_op jit(solution)/shard_map/reduce_scatter | solution.py:288
  (1302 shorter events, 610.8 us)
Async XLA Ops:
  8.0 353.4 %reduce-scatter.6.cloned.1.call-start = ((), (), s32[]{:S(2)}) async-start(), calls=%async_computation.6 | async-start | bytes 5898240 | tf_op jit(solution)/shard_map/reduce_scatter | solution.py:193
  93.0 31.6 %copy-start.126 = (f32[3,33]{1,0:T(4,128)S(1)}, f32[3,33]{1,0:T(4,128)}, u32[]{:S(2)}) copy-start(f32[3,33]{1,0:T(4,128)} %copy-done.125) | copy-start | bytes 1192 | tf_op jit(solution)/shard_map/jvp()/while
  269.7 91.8 %copy-start.95 = (f32[768]{0:T(1024)S(1)}, f32[768]{0:T(1024)}, u32[]{:S(2)}) copy-start(f32[768]{0:T(1024)} %param.27) | copy-start | bytes 9220
  269.7 135.4 %all-gather.4.cloned.1.call-start = ((), (), s32[]{:S(2)}) async-start(), calls=%async_computation.7 | async-start | bytes 4866048 | tf_op jit(solution)/shard_map/all_gather | solution.py:204
  270.3 199.3 %all-gather.6.cloned.1.call-start = ((), (), s32[]{:S(2)}) async-start(), calls=%async_computation.8 | async-start | bytes 4866048 | tf_op jit(solution)/shard_map/all_gather | solution.py:206
  270.9 327.4 %all-gather.8.cloned.1.call-start = ((), (), s32[]{:S(2)}) async-start(), calls=%async_computation.9 | async-start | bytes 5898240 | tf_op jit(solution)/shard_map/all_gather | solution.py:238
  318.1 87.0 %copy-start.121 = (f32[768]{0:T(1024)S(1)}, f32[768]{0:T(1024)}, u32[]{:S(2)}) copy-start(f32[768]{0:T(1024)} %param.28) | copy-start | bytes 9220
  318.1 87.0 %copy-start.130 = (f32[768]{0:T(1024)S(1)}, f32[768]{0:T(1024)}, u32[]{:S(2)}) copy-start(f32[768]{0:T(1024)} %param.29) | copy-start | bytes 9220
  363.7 142.1 %copy-start.99 = (f32[768]{0:T(1024)}, f32[768]{0:T(1024)S(1)}, u32[]{:S(2)}) copy-start(f32[768]{0:T(1024)S(1)} %broadcast_multiply_fusion.5) | copy-start | bytes 9220
  365.6 140.1 %copy-start.106 = (f32[768]{0:T(1024)}, f32[768]{0:T(1024)S(1)}, u32[]{:S(2)}) copy-start(f32[768]{0:T(1024)S(1)} %fusion.363) | copy-start | bytes 9220
  365.6 103.9 %copy-start.129 = (f32[768]{0:T(1024)S(1)}, f32[768]{0:T(1024)}, u32[]{:S(2)}) copy-start(f32[768]{0:T(1024)} %param.33) | copy-start | bytes 9220
  510.3 688.6 %reduce-scatter.8.cloned.1.call-start = ((), (), s32[]{:S(2)}) async-start(), calls=%async_computation.10 | async-start | bytes 5898240 | tf_op jit(solution)/shard_map/reduce_scatter | solution.py:263
  656.6 41.9 %copy-start.87 = (f32[192]{0:T(256)}, f32[192]{0:T(256)S(1)}, u32[]{:S(2)}) copy-start(f32[192]{0:T(256)S(1)} %get-tuple-element.2549) | copy-start | bytes 2308 | tf_op jit(solution)/shard_map/transpose(jvp())/while
  657.1 41.5 %copy-start.91 = (f32[192]{0:T(256)}, f32[192]{0:T(256)S(1)}, u32[]{:S(2)}) copy-start(f32[192]{0:T(256)S(1)} %fusion.1098) | copy-start | bytes 2308 | tf_op jit(solution)/shard_map/transpose(jvp())/while
  811.4 41.7 %copy-start.87 = (f32[192]{0:T(256)}, f32[192]{0:T(256)S(1)}, u32[]{:S(2)}) copy-start(f32[192]{0:T(256)S(1)} %get-tuple-element.2549) | copy-start | bytes 2308 | tf_op jit(solution)/shard_map/transpose(jvp())/while
  811.9 41.2 %copy-start.91 = (f32[192]{0:T(256)}, f32[192]{0:T(256)S(1)}, u32[]{:S(2)}) copy-start(f32[192]{0:T(256)S(1)} %fusion.1098) | copy-start | bytes 2308 | tf_op jit(solution)/shard_map/transpose(jvp())/while
  965.9 41.9 %copy-start.87 = (f32[192]{0:T(256)}, f32[192]{0:T(256)S(1)}, u32[]{:S(2)}) copy-start(f32[192]{0:T(256)S(1)} %get-tuple-element.2549) | copy-start | bytes 2308 | tf_op jit(solution)/shard_map/transpose(jvp())/while
  966.4 41.4 %copy-start.91 = (f32[192]{0:T(256)}, f32[192]{0:T(256)S(1)}, u32[]{:S(2)}) copy-start(f32[192]{0:T(256)S(1)} %fusion.1098) | copy-start | bytes 2308 | tf_op jit(solution)/shard_map/transpose(jvp())/while
  1089.4 227.6 %reduce-scatter.10.cloned.1.call-start = ((), (), s32[]{:S(2)}) async-start(), calls=%async_computation.11 | async-start | bytes 9732096 | tf_op jit(solution)/shard_map/reduce_scatter | solution.py:286
  1101.2 357.5 %reduce-scatter.12.cloned.1.call-start = ((), (), s32[]{:S(2)}) async-start(), calls=%async_computation.12 | async-start | bytes 9732096 | tf_op jit(solution)/shard_map/reduce_scatter | solution.py:288
  1118.5 15.5 %all-to-all-start.1 = ((bf16[8,192,96]{2,1,0:T(8,128)(2,1)}), bf16[8,192,96]{2,1,0:T(8,128)(2,1)S(1)}, u32[]{:S(2)}, u32[]{:S(2)}) async-start(bf16[8,192,96]{2,1,0:T(8,128)(2,1)} %bitcast.526), calls=%async_computation.3 | async-start | bytes 786432 | tf_op jit(solution)/shard_map/all_to_all | solution.py:26
  1134.8 61.6 %all-to-all-start = ((bf16[8,96,3,192]{1,3,2,0:T(8,128)(2,1)}), bf16[8,96,3,192]{1,3,2,0:T(8,128)(2,1)}, u32[]{:S(2)}, u32[]{:S(2)}) async-start(bf16[8,96,3,192]{1,3,2,0:T(8,128)(2,1)} %copy.217), calls=%async_computation.2 | async-start | bytes 2359296 | tf_op jit(solution)/shard_map/all_to_all | solution.py:26
  1139.1 59.8 %copy-start.30 = (f32[768,768]{1,0:T(8,128)S(1)}, f32[768,768]{1,0:T(8,128)}, u32[]{:S(2)}) copy-start(f32[768,768]{1,0:T(8,128)} %copy-done.29) | copy-start | bytes 7077892
  1139.1 59.8 %copy-start.98 = (f32[768]{0:T(1024)S(1)}, f32[768]{0:T(1024)}, u32[]{:S(2)}) copy-start(f32[768]{0:T(1024)} %copy-done.97) | copy-start | bytes 9220
  (312 other events, 2081.0 us)
Sparse Core Ops, SparseCore 0:
  269.8 91.6 reduce-scatter.5
  510.4 87.7 all-gather.7
  1089.5 84.3 reduce-scatter.7
  1180.2 136.7 reduce-scatter.9
  1323.3 135.3 reduce-scatter.11
Sparse Core Ops, SparseCore 1:
  273.0 132.1 all-gather.3
  407.8 61.7 all-gather.5
where the time goes:
time: 1470 us
  matrix products  475 us (32%)
  waiting for transfers between devices  463 us (31%)
  other arithmetic  280 us (19%)
  blocking collectives  96.3 us (7%)
  local copies, waits for them, and re-layouts  95.3 us (6%)
  loops' own time  30 us (2%)
  between operations  19.2 us (1%)
    reduce_scatter x1, waiting for transfers between devices, body(): lax.psum_scatter(down_term, ('batch', 'heads'), scatter_dimension=0, tile...  142 us
    reduce_scatter x1, waiting for transfers between devices, body(): lax.psum_scatter(up_term, ('batch', 'heads'), scatter_dimension=1, tiled=...  115 us
    dot_general x9, matrix products, head_mix(): attended = jnp.dot(first_kernel, mixed_marks, precision=best_precision)  111 us
    reduce_sum x21, other arithmetic, head_mix(): conv_taps[tap_index] * padded_v[tap_index:tap_index + tok_count]  95.5 us
    all_gather x1, waiting for transfers between devices, body(): piece_rows = lax.all_gather(grad_attn_low, 'heads', axis=0, tiled=True)  87.9 us
    dot_general x288, matrix products, batch_mul(): jnp.einsum('...ij,...jk->...ik', left, right, precision=best_precision)  85.9 us
    broadcast_in_dim x3, other arithmetic, heads_mix(): lax.map(jax.checkpoint(one_head), (split_heads(q_all), split_heads(k_all)...  62.2 us
    psum x1, blocking collectives, body(): lax.psum((conv_full, bias_full, bound_total, live_count), ('batch', 'head...  49.4 us
  transfers between devices with their start and end apart: 9, of which 6 were waited for; matrix products, arithmetic and copies ran while one was open for 6% of the time, Pallas kernels for 0%

commit v1 on v0

v1 whole, which is shorter than its diff:
```python
from functools import partial

import jax
import jax.numpy as jnp
from jax import lax
from jax.experimental import pallas as pl
from jax.experimental.pallas import tpu as pltpu
from jax.sharding import PartitionSpec as P

HEAD_DIM = 64
PINV_ITERS = 6
SUB = 256
HALO = 128
f32 = jnp.float32
bf16 = jnp.bfloat16
mask_fill = -1000000000.0
norm_eps = 1e-05
contract_rows = (((0,), (0,)), ((), ()))
contract_cols = (((1,), (1,)), ((), ()))


def mul(a, b, ca, cb):
    return lax.dot_general(a, b, (((ca,), (cb,)), ((), ())), preferred_element_type=f32)


def halves(x):
    high = x.astype(bf16)
    return high, (x - high.astype(f32)).astype(bf16)


def mul3(a, b, ca, cb):
    ah, al = halves(a)
    bh, bl = halves(b)
    return mul(ah, bh, ca, cb) + (mul(ah, bl, ca, cb) + mul(al, bh, ca, cb))


def band_of(row):
    wide = jnp.broadcast_to(row, (2 * SUB, 2 * SUB))
    return pltpu.roll(wide, 0, 1, stride=1, stride_axis=0)[:, :SUB].astype(bf16)


def softmax_down(scores):
    top = jnp.max(scores, axis=0, keepdims=True)
    e = jnp.exp(scores - top)
    return e, 1.0 / jnp.sum(e, axis=0, keepdims=True)


def softmax_across(scores):
    e = jnp.exp(scores - jnp.max(scores, axis=1, keepdims=True))
    return e / jnp.sum(e, axis=1, keepdims=True)


def forward_kernel(len_ref, start_ref, lo_ref, hi_ref, inv_ref, taps_ref, qkv_ref,
                   out_ref, marks_ref, lse_ref, square_ref, newton_ref, bound_ref, padded, band, acc):
    heads = taps_ref.shape[0]
    width = heads * HEAD_DIM
    tokens = qkv_ref.shape[1]
    block = out_ref.shape[2]
    marks = lo_ref.shape[0] // len_ref.shape[0]
    root = HEAD_DIM ** (-0.25)
    at = [slice(h * HEAD_DIM, (h + 1) * HEAD_DIM) for h in range(heads)]
    every = range(heads)

    out_ref[...] = jnp.zeros_like(out_ref)
    bound_ref[...] = jnp.zeros_like(bound_ref)
    padded[:, :HALO] = jnp.zeros((width, HALO), bf16)
    padded[:, HALO + tokens:] = jnp.zeros((width, HALO), bf16)
    padded[:, HALO:HALO + tokens] = qkv_ref[2 * width:, :]
    for h in every:
        band[h] = band_of(taps_ref[h:h + 1, :])

    def per_slot(s, carry):
        count, start = len_ref[s], start_ref[s]

        @pl.when(count > 0)
        def _():
            lo = lo_ref[pl.ds(s * marks, marks), :]
            hi = hi_ref[pl.ds(s * marks, marks), :]
            inv = inv_ref[pl.ds(s, 1), :]
            first, last = start // block, (start + count - 1) // block + 1

            def lanes(i):
                return pl.ds(pl.multiple_of(i * block, block), block)

            def token(i):
                return i * block + lax.broadcasted_iota(jnp.int32, (1, block), 1)

            def live(i):
                t = token(i)
                return (t >= start) & (t < start + count)

            acc[...] = jnp.zeros_like(acc)

            def mark_sums(i, c):
                t = token(i)
                member = ((t >= lo) & (t < hi)).astype(f32).astype(bf16)
                acc[...] += mul(qkv_ref[:2 * width, lanes(i)], member, 1, 1)
                return c

            lax.fori_loop(first, last, mark_sums, 0)
            both = acc[...] * inv * root
            marks_ref[s] = both
            ql = [both[at[h]].T for h in every]
            klt = [both[width + h * HEAD_DIM:width + (h + 1) * HEAD_DIM] for h in every]
            middle = [softmax_across(mul3(ql[h], klt[h], 1, 0)) for h in every]
            bound = [jnp.max(jnp.sum(a, axis=0, keepdims=True), axis=1, keepdims=True) for a in middle]
            bound_ref[...] += sum(bound)

            def sweep(it, inverse):
                product = [mul3(middle[h], inverse[h], 1, 0) for h in every]
                side = [mul3(inverse[h], product[h], 1, 0) for h in every]
                poly = [7.0 * product[h] - mul3(product[h], product[h], 1, 0) for h in every]
                for h in every:
                    newton_ref[s, it, 0, h] = inverse[h]
                    newton_ref[s, it, 1, h] = product[h]
                    newton_ref[s, it, 2, h] = side[h]
                    newton_ref[s, it, 3, h] = poly[h]
                return tuple(
                    0.25 * (13.0 * inverse[h] - 15.0 * side[h] + mul3(side[h], poly[h], 1, 0)) for h in every
                )

            inverse = lax.fori_loop(0, PINV_ITERS, sweep, tuple(middle[h].T / bound[h] for h in every))

            query = [(ql[h] * root).astype(bf16) for h in every]

            def scores(i, h):
                key = qkv_ref[width + h * HEAD_DIM:width + (h + 1) * HEAD_DIM, lanes(i)]
                return jnp.where(live(i), mul(query[h], key, 1, 0), mask_fill)

            def find_top(i, tops):
                return tuple(jnp.maximum(tops[h], jnp.max(scores(i, h), axis=1, keepdims=True)) for h in every)

            tops = lax.fori_loop(first, last, find_top, tuple(jnp.full((marks, 1), mask_fill, f32) for _ in every))

            def gather(i, sums):
                out = []
                for h in every:
                    e = jnp.exp(scores(i, h) - tops[h])
                    value = qkv_ref[2 * width + h * HEAD_DIM:2 * width + (h + 1) * HEAD_DIM, lanes(i)]
                    acc[at[h], :] += mul(e.astype(bf16), value, 1, 1)
                    out.append(sums[h] + jnp.sum(e, axis=1, keepdims=True))
                return tuple(out)

            acc[...] = jnp.zeros_like(acc)
            sums = lax.fori_loop(first, last, gather, tuple(jnp.zeros((marks, 1), f32) for _ in every))
            values = [acc[at[h], :] / sums[h] for h in every]
            mixed = [mul3(inverse[h], values[h], 1, 0) for h in every]
            for h in every:
                lse_ref[s, h] = tops[h] + jnp.log(sums[h])
                square_ref[s, 0, h] = middle[h]
                square_ref[s, 1, h] = inverse[h]
                square_ref[s, 2, h] = values[h]
                square_ref[s, 3, h] = mixed[h]
            mixed_t = [mixed[h].T.astype(bf16) for h in every]
            kl = [(klt[h].T * root).astype(bf16) for h in every]

            def finish(i, c):
                for h in every:
                    e, scale = softmax_down(mul(kl[h], qkv_ref[at[h], lanes(i)], 1, 0))
                    rows = mul(mixed_t[h], e.astype(bf16), 1, 0) * scale
                    conv = []
                    for sub in range(block // SUB):
                        left = i * block + sub * SUB
                        t = left - HALO + lax.broadcasted_iota(jnp.int32, (1, 2 * SUB), 1)
                        near = padded[at[h], pl.ds(pl.multiple_of(left, SUB), 2 * SUB)].astype(f32)
                        near = jnp.where((t >= start) & (t < start + count), near, 0.0).astype(bf16)
                        conv.append(mul(near, band[h], 1, 0))
                    rows = rows + jnp.concatenate(conv, axis=1)
                    rows = jnp.where(live(i), rows, out_ref[i, at[h], :].astype(f32))
                    out_ref[i, at[h], :] = rows.astype(bf16)
                return c

            lax.fori_loop(first, last, finish, 0)

        return carry

    lax.fori_loop(0, len_ref.shape[0], per_slot, 0)


def backward_kernel(len_ref, start_ref, lo_ref, hi_ref, inv_ref, taps_ref, qkv_ref, grad_ref, marks_ref, lse_ref,
                    square_ref, newton_ref, out_ref, sums_ref, conv_ref, padded_v, padded_g, band, acc, small, cross):
    heads = taps_ref.shape[0]
    taps = conv_ref.shape[1]
    width = heads * HEAD_DIM
    tokens = qkv_ref.shape[1]
    blocks, _, block = grad_ref.shape
    marks = lo_ref.shape[0] // len_ref.shape[0]
    root = HEAD_DIM ** (-0.25)
    at = [slice(h * HEAD_DIM, (h + 1) * HEAD_DIM) for h in range(heads)]
    k_at = [slice(width + h * HEAD_DIM, width + (h + 1) * HEAD_DIM) for h in range(heads)]
    v_at = [slice(2 * width + h * HEAD_DIM, 2 * width + (h + 1) * HEAD_DIM) for h in range(heads)]
    every = range(heads)
    subs = range(block // SUB)

    acc[...] = jnp.zeros_like(acc)
    cross[...] = jnp.zeros_like(cross)
    for buf in (padded_v, padded_g):
        buf[:, :HALO] = jnp.zeros((width, HALO), bf16)
        buf[:, HALO + tokens:] = jnp.zeros((width, HALO), bf16)
    padded_v[:, HALO:HALO + tokens] = qkv_ref[2 * width:, :]
    for i in range(blocks):
        padded_g[:, HALO + i * block:HALO + (i + 1) * block] = grad_ref[i]
    for h in every:
        band[h] = band_of(taps_ref[h:h + 1, :])

    def per_slot(s, carry):
        count, start = len_ref[s], start_ref[s]

        @pl.when(count > 0)
        def _():
            lo = lo_ref[pl.ds(s * marks, marks), :]
            hi = hi_ref[pl.ds(s * marks, marks), :]
            inv = inv_ref[pl.ds(s, 1), :]
            first, last = start // block, (start + count - 1) // block + 1

            def lanes(i):
                return pl.ds(pl.multiple_of(i * block, block), block)

            def token(i):
                return i * block + lax.broadcasted_iota(jnp.int32, (1, block), 1)

            def inside(t):
                return (t >= start) & (t < start + count)

            def near(buf, i, sub, h):
                left = i * block + sub * SUB
                t = left - HALO + lax.broadcasted_iota(jnp.int32, (1, 2 * SUB), 1)
                wide = buf[at[h], pl.ds(pl.multiple_of(left, SUB), 2 * SUB)].astype(f32)
                return jnp.where(inside(t), wide, 0.0).astype(bf16)

            both = marks_ref[s]
            qlt = [both[at[h]] for h in every]
            klt = [both[k_at[h]] for h in every]
            middle = [square_ref[s, 0, h] for h in every]
            inverse = [square_ref[s, 1, h] for h in every]
            values = [square_ref[s, 2, h] for h in every]
            mixed = [square_ref[s, 3, h].astype(bf16) for h in every]
            klt_low = [(klt[h] * root).astype(bf16) for h in every]
            kl_low = [(klt[h].T * root).astype(bf16) for h in every]
            small[...] = jnp.zeros_like(small)

            def first_part(i, c):
                on = inside(token(i))
                for h in every:
                    query = qkv_ref[at[h], lanes(i)]
                    grad = jnp.where(on, grad_ref[i, at[h], :].astype(f32), 0.0).astype(bf16)
                    e, scale = softmax_down(mul(kl_low[h], query, 1, 0))
                    weight = e * scale
                    part = weight * mul(mixed[h], grad, 1, 0)
                    delta = (part - weight * jnp.sum(part, axis=0, keepdims=True)).astype(bf16)
                    small[0, h] += mul(weight.astype(bf16), grad, 1, 1)
                    small[1, h] += mul(query, delta, 1, 1)
                    acc[at[h], lanes(i)] += mul(klt_low[h], delta, 1, 0)
                return c

            lax.fori_loop(first, last, first_part, 0)
            grad_mixed = [small[0, h] for h in every]
            grad_values = [mul3(inverse[h], grad_mixed[h], 0, 0) for h in every]
            grad_inverse = tuple(mul3(grad_mixed[h], values[h], 1, 1) for h in every)

            def sweep(step, pair):
                g, grad_a = pair
                it = PINV_ITERS - 1 - step
                new_g, new_a = [], []
                for h in every:
                    z, x = newton_ref[s, it, 0, h], newton_ref[s, it, 1, h]
                    y, w = newton_ref[s, it, 2, h], newton_ref[s, it, 3, h]
                    quarter = 0.25 * g[h]
                    dy = mul3(quarter, w, 1, 1) - 15.0 * quarter
                    dw = mul3(y, quarter, 0, 0)
                    dx = 7.0 * dw - mul3(dw, x, 1, 1) - mul3(x, dw, 0, 0) + mul3(z, dy, 0, 0)
                    new_g.append(13.0 * quarter + mul3(dy, x, 1, 1) + mul3(middle[h], dx, 0, 0))
                    new_a.append(grad_a[h] + mul3(dx, z, 1, 1))
                return tuple(new_g), tuple(new_a)

            grad_start, grad_middle = lax.fori_loop(
                0, PINV_ITERS, sweep, (grad_inverse, tuple(jnp.zeros((marks, marks), f32) for _ in every))
            )
            for h in every:
                column = jnp.sum(middle[h], axis=0, keepdims=True)
                bound = jnp.max(column, axis=1, keepdims=True)
                back = grad_start[h].T / bound
                total = jnp.sum(jnp.sum(back * middle[h], axis=0, keepdims=True), axis=1, keepdims=True)
                hit = (column == bound).astype(f32)
                share = hit * (-total / bound / jnp.sum(hit, axis=1, keepdims=True))
                grad_a = grad_middle[h] + back + share
                delta = middle[h] * (grad_a - jnp.sum(grad_a * middle[h], axis=1, keepdims=True))
                small[2, h] = mul3(klt[h], delta, 1, 1)
                small[3, h] = mul3(qlt[h], delta, 1, 0)
                small[0, h] = jnp.zeros((marks, marks), f32)
            offset = [jnp.sum(grad_values[h] * values[h], axis=1, keepdims=True) for h in every]
            grad_low = [grad_values[h].astype(bf16) for h in every]
            grad_low_t = [grad_values[h].T.astype(bf16) for h in every]
            qlt_low = [(qlt[h] * root).astype(bf16) for h in every]
            ql_low = [(qlt[h].T * root).astype(bf16) for h in every]

            def second_part(i, c):
                on = inside(token(i))
                for h in every:
                    key, value = qkv_ref[k_at[h], lanes(i)], qkv_ref[v_at[h], lanes(i)]
                    score = jnp.where(on, mul(ql_low[h], key, 1, 0), mask_fill)
                    weight = jnp.exp(score - lse_ref[s, h])
                    delta = (weight * (mul(grad_low[h], value, 1, 0) - offset[h])).astype(bf16)
                    small[0, h] += mul(key, delta, 1, 1)
                    acc[k_at[h], lanes(i)] += mul(qlt_low[h], delta, 1, 0)
                    around_g = [near(padded_g, i, sub, h) for sub in subs]
                    around_v = [near(padded_v, i, sub, h) for sub in subs]
                    conv = jnp.concatenate([mul(g, band[h], 1, 0) for g in around_g], axis=1)
                    acc[v_at[h], lanes(i)] += mul(grad_low_t[h], weight.astype(bf16), 1, 0) + jnp.where(on, conv, 0.0)
                    here = [g[:, HALO:HALO + SUB] for g in around_g]
                    cross[h] += mul(jnp.concatenate(around_v, axis=0), jnp.concatenate(here, axis=0), 0, 0)
                return c

            lax.fori_loop(first, last, second_part, 0)
            scale = inv * root
            spread = [((small[2, h] + root * small[0, h]) * scale).astype(bf16) for h in every]
            spread += [((small[3, h] + root * small[1, h]) * scale).astype(bf16) for h in every]
            spread = jnp.concatenate(spread, axis=0)

            def spread_marks(i, c):
                t = token(i)
                member = ((t >= lo) & (t < hi)).astype(f32).astype(bf16)
                acc[:2 * width, lanes(i)] += mul(spread, member, 1, 0)
                return c

            lax.fori_loop(first, last, spread_marks, 0)

        return carry

    lax.fori_loop(0, len_ref.shape[0], per_slot, 0)
    sums_ref[...] = jnp.zeros_like(sums_ref)

    def store(i, c):
        at_lanes = pl.ds(pl.multiple_of(i * block, block), block)
        rounded = acc[:, at_lanes].astype(bf16)
        out_ref[:, at_lanes] = rounded
        sums_ref[...] += jnp.sum(rounded.astype(f32), axis=1, keepdims=True)
        return c

    lax.fori_loop(0, blocks, store, 0)
    low, high = HALO - taps // 2 - 16, HALO + SUB + taps // 2 + 16
    gap = (lax.broadcasted_iota(jnp.int32, (high - low, SUB), 0) + low
           - lax.broadcasted_iota(jnp.int32, (high - low, SUB), 1) - (HALO - taps // 2))
    for h in every:
        zone = cross[h, low:high, :]
        rows = [jnp.sum(jnp.where(gap == i, zone, 0.0), axis=0, keepdims=True) for i in range(taps)]
        conv_ref[h] = jnp.sum(jnp.concatenate(rows, axis=0), axis=1, keepdims=True)


def laid_taps(taps, half):
    heads, n = taps.shape
    room = 2 * SUB - (HALO - half) - (n - 1)
    return jnp.pad(taps[:, ::-1], ((0, 0), (room, 2 * SUB - room - n)))


def layout_of(lengths, bounds):
    lengths = lengths.astype(jnp.int32)
    starts = jnp.cumsum(lengths) - lengths
    upper = jnp.concatenate([bounds[:, 1:], lengths[:, None]], axis=1)
    lo = (bounds + starts[:, None]).reshape(-1, 1)
    hi = (upper + starts[:, None]).reshape(-1, 1)
    inv = 1.0 / jnp.maximum((upper - bounds).astype(f32), 1.0)
    return lengths, starts, lo, hi, inv


def specs(*kinds):
    return [pl.BlockSpec(memory_space=pltpu.SMEM if k == "s" else pltpu.VMEM) for k in kinds]


VMEM_LIMIT = 62 * 1024 * 1024


def attention_forward(layout, taps, qkv, blocks):
    lengths, starts, lo, hi, inv = layout
    slots, marks = inv.shape
    heads, n = taps.shape
    width, tokens = heads * HEAD_DIM, qkv.shape[1]
    shape = jax.ShapeDtypeStruct
    return pl.pallas_call(
        forward_kernel,
        name="attention_forward",
        out_shape=(
            shape((blocks, width, tokens // blocks), bf16),
            shape((slots, 2 * width, marks), f32),
            shape((slots, heads, marks, 1), f32),
            shape((slots, 4, heads, marks, marks), f32),
            shape((slots, PINV_ITERS, 4, heads, marks, marks), f32),
            shape((1, 1), f32),
        ),
        in_specs=specs("s", "s", "v", "v", "v", "v", "v"),
        out_specs=specs(*"vvvvvv"),
        scratch_shapes=[
            pltpu.VMEM((width, tokens + 2 * HALO), bf16),
            pltpu.VMEM((heads, 2 * SUB, SUB), bf16),
            pltpu.VMEM((2 * width, marks), f32),
        ],
        cost_estimate=pl.CostEstimate(flops=20_000_000_000, bytes_accessed=12_000_000, transcendentals=2_000_000),
        compiler_params=pltpu.CompilerParams(vmem_limit_bytes=VMEM_LIMIT),
    )(lengths, starts, lo, hi, inv, laid_taps(taps, n // 2), qkv)


def attention_backward(layout, taps, qkv, grad, saved):
    lengths, starts, lo, hi, inv = layout
    slots, marks = inv.shape
    heads, n = taps.shape
    width, tokens = heads * HEAD_DIM, qkv.shape[1]
    shape = jax.ShapeDtypeStruct
    return pl.pallas_call(
        backward_kernel,
        name="attention_backward",
        out_shape=(
            shape((3 * width, tokens), bf16),
            shape((3 * width, 1), f32),
            shape((heads, n, 1), f32),
        ),
        in_specs=specs(*"ssvvvvvvvvvv"),
        out_specs=specs(*"vvv"),
        scratch_shapes=[
            pltpu.VMEM((width, tokens + 2 * HALO), bf16),
            pltpu.VMEM((width, tokens + 2 * HALO), bf16),
            pltpu.VMEM((heads, 2 * SUB, SUB), bf16),
            pltpu.VMEM((3 * width, tokens), f32),
            pltpu.VMEM((4, heads, marks, marks), f32),
            pltpu.VMEM((heads, 2 * SUB, SUB), f32),
        ],
        cost_estimate=pl.CostEstimate(flops=50_000_000_000, bytes_accessed=18_000_000, transcendentals=2_000_000),
        compiler_params=pltpu.CompilerParams(vmem_limit_bytes=VMEM_LIMIT),
    )(lengths, starts, lo, hi, inv, laid_taps(taps[:, ::-1], n // 2), qkv, grad, *saved)


def layer_norm(row_data, gain_vec, shift_vec):
    centre = row_data - jnp.mean(row_data, axis=1, keepdims=True)
    spread = jnp.mean(centre * centre, axis=1, keepdims=True)
    return centre * lax.rsqrt(spread + norm_eps) * gain_vec[None, :] + shift_vec[None, :]


def gelu_exact(values):
    return jax.nn.gelu(values, approximate=False)


def widened(rows, width):
    return jnp.pad(rows, ((0, 0),) * (rows.ndim - 1) + ((0, width - rows.shape[-1]),))


def swap(x, mask):
    size = lax.axis_size("batch")
    return lax.ppermute(x, "batch", [(i, i ^ mask) for i in range(size)])


def joined(a, b):
    return (a.astype(f32) + b.astype(f32)).astype(bf16)


def bits_of(size):
    return [1 << k for k in range(size.bit_length() - 1)]


def place_of(size):
    if size == 1:
        return [0]
    return [((p & (size // 2 - 1)) << 1) | (p // (size // 2)) for p in range(size)]


def gather_relative(block, order, size):
    pieces = {0: block}
    for mask in order:
        pieces.update({key ^ mask: swap(piece, mask) for key, piece in list(pieces.items())})
    return [pieces[key] for key in place_of(size)]


def scatter_relative(pieces, order):
    for mask in order:
        pieces = {key: joined(piece, swap(pieces[key ^ mask], mask)) for key, piece in pieces.items() if not key & mask}
    return pieces[0]


def across_heads(x):
    return lax.all_to_all(x, "heads", 0, 0, tiled=True)


def sum_over_line(blocks):
    size = blocks.shape[0]
    here = lax.axis_index("heads")

    def pick(at):
        return lax.dynamic_index_in_dim(blocks, jnp.clip(at, 0, size - 1), 0, keepdims=False)

    up = down = None
    for k in range(1, size):
        send_up, send_down = pick(size - k + here), pick(k - size + here)
        if k > 1:
            send_up, send_down = joined(send_up, up), joined(send_down, down)
        up = lax.ppermute(send_up, "heads", [(h, h + 1) for h in range(k)])
        down = lax.ppermute(send_down, "heads", [(size - 1 - h, size - 2 - h) for h in range(k)])
    total = pick(here).astype(f32)
    return total if up is None else total + up.astype(f32) + down.astype(f32)


def body(
    tokens,
    qkv_weight,
    qv_bias,
    conv_weight,
    out_weight,
    out_bias,
    norm1_gain,
    norm1_bias,
    ffn_in_weight,
    ffn_in_bias,
    ffn_out_weight,
    ffn_out_bias,
    norm2_gain,
    norm2_bias,
    cotangent,
    seq_lengths,
    segment_ids,
    landmark_bounds,
):
    tok_count, model_width = tokens.shape
    head_width = qkv_weight.shape[2]
    heads_here = head_width // HEAD_DIM
    head_total, taps = conv_weight.shape
    groups, packs = lax.axis_size("heads"), lax.axis_size("batch")
    devices = groups * packs
    quarter = tok_count // groups
    ffn_own = ffn_in_bias.shape[0]
    ffn_all = ffn_own * devices
    head_index = lax.axis_index("heads")

    places = place_of(packs)
    bits = bits_of(packs)
    rising, falling = bits[1:] + bits[:1], bits[1:][::-1] + bits[:1]

    def shared(x):
        return across_heads(jnp.broadcast_to(x[None], (groups, *x.shape)))

    def whole_of(x, order):
        return jnp.concatenate(gather_relative(shared(x), order, packs), axis=0)

    whole_in = whole_of(ffn_in_weight.T, rising).reshape(ffn_all, model_width)
    whole_in_bias = whole_of(ffn_in_bias, falling).reshape(ffn_all)
    whole_out = whole_of(ffn_out_weight, falling).reshape(ffn_all, model_width)
    whole_attn = shared(out_weight).reshape(groups * head_width, model_width)

    layout = layout_of(seq_lengths, landmark_bounds)
    own_tokens = lax.dynamic_slice_in_dim(tokens, head_index * quarter, quarter, 0).astype(f32)
    conv_own = lax.dynamic_slice_in_dim(conv_weight, head_index * heads_here, heads_here, 0)
    qv_own = lax.dynamic_slice_in_dim(qv_bias, head_index * head_width, head_width, 1)
    flat_qkv = qkv_weight.reshape(model_width, 3 * head_width)
    bias_column = jnp.concatenate([qv_own[0], jnp.zeros_like(qv_own[0]), qv_own[1]])
    qkv = (
        lax.dot_general(flat_qkv, tokens, (((0,), (1,)), ((), ())), preferred_element_type=f32)
        + bias_column[:, None]
    ).astype(bf16)
    mixed, *saved, bound = attention_forward(layout, conv_own, qkv, groups)
    mixed = lax.all_to_all(mixed, "heads", 0, 0, tiled=True).reshape(groups * head_width, quarter)
    attn = lax.dot_general(mixed, whole_attn, contract_rows, preferred_element_type=f32)
    first_res = own_tokens + attn + out_bias[None, :]
    norm1_out, norm1_pull = jax.vjp(layer_norm, first_res, norm1_gain, norm1_bias)
    norm1_low = norm1_out.astype(bf16)
    pre_act = (
        lax.dot_general(norm1_low, whole_in, contract_cols, preferred_element_type=f32)
        + whole_in_bias.astype(f32)[None, :]
    )
    hidden_act, gelu_pull = jax.vjp(gelu_exact, pre_act)
    hidden_low = hidden_act.astype(bf16)
    ffn_result = jnp.dot(hidden_low, whole_out, preferred_element_type=f32) + ffn_out_bias[None, :]
    final_out, norm2_pull = jax.vjp(layer_norm, norm1_out + ffn_result, norm2_gain, norm2_bias)
    grad_second, grad_gain_two, grad_shift_two = norm2_pull(cotangent.astype(f32))
    grad_ffn_low = grad_second.astype(bf16)
    grad_ffn_bias = jnp.sum(grad_ffn_low.astype(f32), axis=0)

    def summed_to_owner(left, right, order):
        half = ffn_all // 2
        away = lax.dot_general(left[:, half:], right, contract_rows, preferred_element_type=f32).astype(bf16)
        away = swap(away, bits[0])
        kept = lax.dot_general(left[:, :half], right, contract_rows, preferred_element_type=f32)
        kept = (kept + away.astype(f32)).astype(bf16).reshape(packs // 2, groups, ffn_own, model_width)
        return scatter_relative({places[p]: kept[p] for p in range(packs // 2)}, order[:-1])

    down_block = summed_to_owner(hidden_low, grad_ffn_low, rising)
    grad_hidden = lax.dot_general(grad_ffn_low, whole_out, contract_cols, preferred_element_type=f32)
    grad_pre = gelu_pull(grad_hidden)[0].astype(bf16)
    grad_in_bias = jnp.sum(grad_pre.astype(f32), axis=0)
    up_block = summed_to_owner(grad_pre, norm1_low, falling)
    grad_norm1 = grad_second + jnp.dot(grad_pre, whole_in, preferred_element_type=f32)
    grad_first, grad_gain_one, grad_shift_one = norm1_pull(grad_norm1)
    grad_attn = grad_first.astype(bf16)
    grad_out_bias = jnp.sum(grad_attn.astype(f32), axis=0)
    grad_mix = lax.dot_general(whole_attn, grad_attn, contract_cols, preferred_element_type=f32).astype(bf16)
    grad_mix = lax.all_to_all(grad_mix.reshape(groups, head_width, quarter), "heads", 0, 0, tiled=True)
    out_part = lax.dot_general(
        grad_attn, mixed, (((0,), (1,)), ((), ())), preferred_element_type=f32
    ).astype(bf16)

    vector_all = jnp.stack(
        [grad_ffn_bias, grad_gain_two, grad_shift_two, grad_gain_one, grad_shift_one, grad_out_bias]
    )
    vector_own = model_width // devices
    pack_cols = model_width // packs
    live_slots = jnp.where(head_index == 0, jnp.sum((seq_lengths > 0).astype(f32)), 0.0)
    spot = [places.index(mask) for mask in range(packs)]
    absolute = jnp.asarray(spot, jnp.int32)[jnp.arange(packs) ^ lax.axis_index("batch")]
    extras = jnp.concatenate(
        [
            jnp.take(grad_in_bias.reshape(packs, groups, ffn_own), absolute, axis=0),
            jnp.transpose(vector_all.reshape(6, packs, groups, vector_own), (1, 2, 0, 3)).reshape(
                packs, groups, 6 * vector_own
            ),
            jnp.broadcast_to(jnp.stack([bound[0, 0], live_slots]), (packs, groups, 2)),
        ],
        axis=2,
    )
    extras = jnp.sum(lax.all_to_all(extras, "batch", 0, 0, tiled=True), axis=0)
    extra = jnp.sum(across_heads(extras), axis=0)
    out_block = lax.all_to_all(out_part.reshape(packs, pack_cols, model_width), "batch", 0, 0, tiled=True)
    out_block = jnp.sum(out_block.astype(f32), axis=0).astype(bf16)
    out_block = jnp.transpose(out_block.reshape(pack_cols, groups, head_width), (1, 0, 2))
    out_share = jnp.sum(across_heads(out_block).astype(f32), axis=0).T

    grad_qkv, row_sums, grad_conv = attention_backward(layout, conv_own, qkv, grad_mix, saved)
    qkv_part = lax.dot_general(
        tokens, grad_qkv, (((0,), (1,)), ((), ())), preferred_element_type=f32
    ).astype(bf16)
    input_part = lax.dot_general(
        grad_qkv, flat_qkv, (((0,), (1,)), ((), ())), preferred_element_type=f32
    ).astype(bf16)
    input_grad = grad_first + sum_over_line(input_part.reshape(groups, quarter, model_width))
    down_share = jnp.sum(across_heads(down_block).astype(f32), axis=0)
    up_share = jnp.sum(across_heads(up_block).astype(f32), axis=0).T
    sums = row_sums[:, 0]
    common = jnp.concatenate([sums[:head_width], sums[2 * head_width :], grad_conv.reshape(-1)])
    pack_rows = model_width // packs
    rows_qkv = -(-(pack_rows + 1) // 16) * 16
    qkv_send = jnp.concatenate(
        [
            qkv_part.reshape(packs, pack_rows, 3 * head_width),
            jnp.broadcast_to(widened(common[None], 3 * head_width).astype(bf16), (packs, 1, 3 * head_width)),
            jnp.zeros((packs, rows_qkv - pack_rows - 1, 3 * head_width), bf16),
        ],
        axis=1,
    )
    qkv_total = jnp.sum(lax.all_to_all(qkv_send, "batch", 0, 0, tiled=True).astype(f32), axis=0)
    common = qkv_total[pack_rows]
    at_bound = ffn_own + 6 * vector_own
    return (
        final_out.astype(bf16),
        input_grad,
        qkv_total[:pack_rows].reshape(pack_rows, 3, head_width),
        common[: 2 * head_width].reshape(2, head_width),
        common[2 * head_width : 2 * head_width + heads_here * taps].reshape(heads_here, taps),
        out_share,
        up_share,
        extra[:ffn_own],
        down_share,
        extra[ffn_own:at_bound].reshape(6, vector_own),
        extra[at_bound] / (extra[at_bound + 1] * head_total),
    )


def solution(mesh):
    in_specs = (
        P("batch", None),
        P(None, None, "heads"),
        P(),
        P(),
        P("heads", None),
        P(),
        P(),
        P(),
        P(None, ("batch", "heads")),
        P(("batch", "heads")),
        P(("batch", "heads"), None),
        P(),
        P(),
        P(),
        P(("batch", "heads"), None),
        P("batch"),
        P("batch"),
        P("batch", None),
    )
    out_specs = (
        P(("batch", "heads"), None),
        P(("batch", "heads"), None),
        P("batch", None, "heads"),
        P(None, "heads"),
        P("heads", None),
        P("heads", "batch"),
        P(None, ("batch", "heads")),
        P(("batch", "heads")),
        P(("batch", "heads"), None),
        P(None, ("batch", "heads")),
        P(),
    )
    return jax.shard_map(body, mesh=mesh, in_specs=in_specs, out_specs=out_specs, check_vma=False)
```

time: 1470 us -> 532 us (0.36)
  matrix products: 475 us -> 107 us
  waiting for transfers between devices: 463 us -> 110 us
  other arithmetic: 280 us -> 47.2 us
  blocking collectives: 96.3 us -> 0 us
  starting transfers between devices: 8.4 us -> 104 us
  Pallas kernels: 0 us -> 70.6 us
  loops' own time: 30 us -> 0 us
  local copies, waits for them, and re-layouts: 95.3 us -> 79 us
    dot_general x386 -> x13, matrix products: 462 us -> 94.2 us  [the longest x1 27 us: body(): lax.dot_general(norm1_low, whole_in, contract_cols, preferred_element_typ...]
    reduce_scatter x4 -> x0, waiting for transfers between devices: 300 us -> none  [the longest x1 142 us: body(): lax.psum_scatter(down_term, ('batch', 'heads'), scatter_dimension=0, tile...]
    all_gather x3 -> x0, waiting for transfers between devices: 162 us -> none  [the longest x1 87.9 us: body(): piece_rows = lax.all_gather(grad_attn_low, 'heads', axis=0, tiled=True)]
    reduce_sum x56 -> x10, other arithmetic: 119 us -> 9.65 us  [the longest x1 2.14 us: body(): grad_ffn_bias = jnp.sum(grad_ffn_low.astype(f32), axis=0)]
    all_to_all x2 -> x13, waiting for transfers between devices: 0.01 us -> 89 us  [the longest x8 37.2 us: across_heads(): return lax.all_to_all(x, 'heads', 0, 0, tiled=True)]
    pallas_call x0 -> x2, Pallas kernels: none -> 70.6 us  [the longest x1 43.8 us: attention_backward(): pl.pallas_call(backward_kernel, name='attention_backward', out_shape=(sha...]
    broadcast_in_dim x4 -> x0, other arithmetic: 64.2 us -> none  [the longest x3 62.2 us: heads_mix(): lax.map(jax.checkpoint(one_head), (split_heads(q_all), split_heads(k_all)...]
    all_to_all x2 -> x13, starting transfers between devices: 8.11 us -> 60.2 us  [the longest x8 38.5 us: across_heads(): return lax.all_to_all(x, 'heads', 0, 0, tiled=True)]
  transfers between devices with their start and end apart: 9 -> 48, of which waited for: 6 -> 12; matrix products, arithmetic and copies ran while one was open for 6% -> 34% of each run, Pallas kernels for 0% -> 14%
where the time goes in v1:
time: 532 us; the launch traced here: 523 us
  waiting for transfers between devices  110 us (21%)
  matrix products  107 us (20%)
  starting transfers between devices  104 us (20%)
  local copies, waits for them, and re-layouts  79 us (15%)
  Pallas kernels  70.6 us (13%)
  other arithmetic  47.2 us (9%)
    pallas_call x1, Pallas kernels, attention_backward(): pl.pallas_call(backward_kernel, name='attention_backward', out_shape=(sha...  43.8 us
    unnamed x101, local copies, waits for them, and re-layouts  42.1 us
    all_to_all x8, starting transfers between devices, across_heads(): return lax.all_to_all(x, 'heads', 0, 0, tiled=True)  38.5 us
    all_to_all x8, waiting for transfers between devices, across_heads(): return lax.all_to_all(x, 'heads', 0, 0, tiled=True)  37.2 us
    dot_general x1, matrix products, body(): lax.dot_general(norm1_low, whole_in, contract_cols, preferred_element_typ...  27 us
    pallas_call x1, Pallas kernels, attention_forward(): pl.pallas_call(forward_kernel, name='attention_forward', out_shape=(shape...  26.8 us
    all_to_all x1, waiting for transfers between devices, body(): lax.all_to_all(mixed, 'heads', 0, 0, tiled=True)  25.1 us
    ppermute x29, starting transfers between devices, swap(): return lax.ppermute(x, 'batch', [(i, i ^ mask) for i in range(size)])  23.7 us
  transfers between devices with their start and end apart: 48, of which 12 were waited for; matrix products, arithmetic and copies ran while one was open for 34% of the time, Pallas kernels for 14%

profile of v1, /device:TPU:0, one launch (start us, length us, event | category | flops | bytes accessed | tf_op | source)
XLA Modules:
  0.0 522.7 jit_solution(1550236763505545216)
XLA Ops:
  2.0 6.3 %all-to-all-start.3 = ((bf16[4,1,96]{2,1,0:T(2,128)(2,1)}), bf16[4,1,96]{2,1,0:T(2,128)(2,1)S(1)}, u32[]{:S(2)}, u32[]{:S(2)}) async-start(bf16[4,1,96]{2,1,0:T(2,128)(2,1)} %broadcast_in_dim.37), calls=%async_computation.3 | async-start | bytes 4096 | tf_op jit(solution)/shard_map/all_to_all | solution.py:478
  15.9 5.1 all-to-all-start.2
  24.2 6.8 %add_convert_fusion.1.qkv_ref = bf16[576,3072]{1,0:T(8,128)(2,1)} fusion(bf16[768,576]{0,1:T(8,128)(2,1)S(1)} %bitcast.95, bf16[3072,768]{1,0:T(8,128)(2,1)} %param.19, f32[576]{0:T(1024)S(1)} %pad_maximum_fusion), kind=kOutput, calls=%fused_computation.20 | convolution fusion | flops 2721447936 | bytes 9144576 | tf_op jit(solution)/shard_map/dot_general | solution.py:552
  31.0 5.4 %all-to-all-done.2 = bf16[4,96,768]{2,1,0:T(8,128)(2,1)} async-done(((bf16[4,96,768]{2,1,0:T(8,128)(2,1)}), bf16[4,96,768]{2,1,0:T(8,128)(2,1)}, u32[]{:S(2)}, u32[]{:S(2)}) %all-to-all-start.2) | async-done | bytes 589856 | tf_op jit(solution)/shard_map/all_to_all | solution.py:478
  41.4 26.8 %attention_forward.1 = (bf16[4,192,768]{2,1,0:T(8,128)(2,1)}, f32[3,384,64]{2,1,0:T(8,128)}, f32[3,3,64,1]{3,2,1,0:T(8,128)}, f32[3,4,3,64,64]{4,3,2,1,0:T(8,128...) custom-call(s32[3]{0:T(128)} %len_ref.3, s32[3]{0:T(128)} %copy-done.30, s32[192,1]{1,0:T(8,128)} %reshape.353.lo_ref, ...), custom_call_target="tpu_custom_call" | custom-call | flops 20000000000 | bytes 12000000 | tf_op jit(solution)/shard_map/attention_forward/pallas_call | solution.py:379
  68.2 5.2 all-to-all-start
  73.4 25.1 %all-to-all-done = bf16[4,192,768]{2,1,0:T(8,128)(2,1)S(1)} async-done(((bf16[4,192,768]{2,1,0:T(8,128)(2,1)}), bf16[4,192,768]{2,1,0:T(8,128)(2,1)S(1)}, u32[]{:S(2)}, u32[]{:S(2)}) %all-to-all-start) | async-done | bytes 1179680 | tf_op jit(solution)/shard_map/all_to_all | solution.py:556
  118.3 9.0 %collective-permute-done.9 = bf16[4,96]{1,0:T(4,128)(2,1)S(1)} collective-permute-done((bf16[4,96]{1,0:T(4,128)(2,1)S(1)}, bf16[4,96]{1,0:T(4,128)(2,1)S(1)}, u32[]{:S(2)}, u32[]{:S(2)}) %collective-permute-start.9) | collective-permute-done | bytes 800 | tf_op jit(solution)/shard_map/ppermute | solution.py:447
  171.7 27.0 %multiply_convert_fusion = (bf16[768,3072]{1,0:T(8,128)(2,1)S(1)}, f32[768,3072]{1,0:T(8,128)}, f32[768,3072]{1,0:T(8,128)}) fusion(f32[3072]{0:T(1024)S(1)} %reshape.326, bf16[768,768]{0,1:T(8,128)(2,1)S(1)} %fusion.27, bf16[3072,768]{1,0:T(8,128)(2,1)} %bitcast.7), kind=kOutput, calls=%fused_computation.6 | convolution fusion | flops 3779592192 | bytes 29503488 | tf_op jit(solution)/shard_map/dot_general | solution.py:562
  199.6 7.8 %fusion.45 = (f32[768]{0:T(1024)S(1)}, f32[768,768]{0,1:T(8,128)S(1)}) fusion(f32[768]{0:T(1024)S(1)} %copy-done.32, bf16[768,3072]{1,0:T(8,128)(2,1)S(1)} %get-tuple-element.113, bf16[3072,768]{1,0:T(8,128)(2,1)} %bitcast.8, f32[768]{0:T(1024)S(1)} %copy-done.25, f32[768]{0:T(1024)S(1)} %copy-done.24, f32[768]{0:T(1024)S(1)} %fusion.33, ...), kind=kOutput, calls=%fused_computation.161 | convolution fusion | flops 3628006656 | bytes 14174208 | tf_op jit(solution)/shard_map/dot_general | solution.py:567
  211.8 12.5 %convert_reduce_fusion = (f32[3072]{0:T(1024)S(1)}, bf16[768,3072]{1,0:T(8,128)(2,1)S(1)}) fusion(f32[768,3072]{1,0:T(8,128)} %get-tuple-element.114, f32[768,3072]{1,0:T(8,128)} %get-tuple-element.141, f32[3072]{0:T(1024)S(1)} %reshape.326, bf16[768,768]{0,1:T(8,128)(2,1)S(1)} %get-tuple-element.110, bf16[3072,768]{1,0:T(8,128)(2,1)} %bitcast.8), kind=kOutput, calls=%fused_computation.4 | convolution fusion | flops 3663983616 | bytes 29515776 | tf_op jit(solution)/shard_map/dot_general | solution.py:582
  224.3 9.3 %multiply_reduce_fusion = (f32[768]{0:T(1024)S(1)}, f32[768]{0:T(1024)S(1)}, f32[768]{0:T(1024)S(1)}, f32[768,768]{0,1:T(8,128)S(1)}) fusion(f32[768,768]{0,1:T(8,128)S(1)} %get-tuple-element.140, f32[768]{0:T(1024)S(1)} %fusion.33, f32[768]{0:T(1024)S(1)} %broadcast_multiply_fusion.1, f32[768]{0:T(1024)S(1)} %copy-done.24, ...), kind=kOutput, calls=%fused_computation.55 | convolution fusion | flops 3633903360 | bytes 17728512 | tf_op jit(solution)/shard_map/dot_general | solution.py:586
  253.4 13.3 %all-to-all-done.7 = bf16[8,96,768]{2,1,0:T(8,128)(2,1)S(1)} async-done(((bf16[8,96,768]{2,1,0:T(8,128)(2,1)}), bf16[8,96,768]{2,1,0:T(8,128)(2,1)S(1)}, u32[]{:S(2)}, u32[]{:S(2)}) %all-to-all-start.7) | async-done | bytes 1179680 | tf_op jit(solution)/shard_map/all_to_all | solution.py:616
  272.5 5.3 %convolution_convert_fusion.2 = bf16[1536,768]{1,0:T(8,128)(2,1)} fusion(bf16[768,768]{0,1:T(8,128)(2,1)S(1)} %copy-done.8, bf16[768,3072]{1,0:T(8,128)(2,1)} %copy-done.34), kind=kOutput, calls=%fused_computation.30 | convolution fusion | flops 1813118976 | bytes 5898240 | tf_op jit(solution)/shard_map/dot_general | solution.py:575
  277.8 5.1 convolution_convert_fusion.1
  285.2 12.4 %all-to-all-done.5.grad_ref = bf16[4,192,768]{2,1,0:T(8,128)(2,1)} async-done(((bf16[4,192,768]{2,1,0:T(8,128)(2,1)}), bf16[4,192,768]{2,1,0:T(8,128)(2,1)}, u32[]{:S(2)}, u32[]{:S(2)}) %all-to-all-start.5) | async-done | bytes 1179680 | tf_op jit(solution)/shard_map/all_to_all | solution.py:591
  300.8 43.8 %attention_backward.1 = (bf16[576,3072]{1,0:T(8,128)(2,1)}, f32[576,1]{1,0:T(8,128)}, f32[3,33,1]{2,1,0:T(8,128)}) custom-call(s32[3]{0:T(128)} %len_ref.3, s32[3]{0:T(128)} %copy-done.30, s32[192,1]{1,0:T(8,128)} %reshape.353.lo_ref, s32[192,1]{1,0:T(8,128)} %add.240.hi_ref, f32[3,64]{1,0:T(4,128)} %maximum_divide_fusion.inv_ref, f32[3,512]{1,0:T(4,128)} %pad.13.taps_ref, ...), custom_call_target="tpu_custom_call" | custom-call | flops 49999998976 | bytes 18000000 | tf_op jit(solution)/shard_map/attention_backward/pallas_call | solution.py:408
  344.6 6.4 %convolution_convert_fusion = bf16[3072,768]{1,0:T(8,128)(2,1)S(1)} fusion(bf16[576,3072]{1,0:T(8,128)(2,1)} %get-tuple-element.25, bf16[768,576]{0,1:T(8,128)(2,1)S(1)} %bitcast.96), kind=kOutput, calls=%fused_computation.21 | convolution fusion | flops 2720268288 | bytes 9142272 | tf_op jit(solution)/shard_map/dot_general | solution.py:625
  369.1 7.2 %fusion.28 = bf16[768,576]{0,1:T(8,128)(2,1)} fusion(bf16[576,3072]{1,0:T(8,128)(2,1)} %get-tuple-element.25, bf16[3072,768]{1,0:T(8,128)(2,1)} %param.19), kind=kOutput, calls=%fused_computation.71 | convolution fusion | flops 2718351360 | bytes 9142272 | tf_op jit(solution)/shard_map/dot_general | solution.py:622
  409.8 21.6 %all-to-all-done.8 = bf16[4,96,192]{2,1,0:T(8,128)(2,1)S(1)} async-done(((bf16[4,96,192]{2,1,0:T(8,128)(2,1)}), bf16[4,96,192]{2,1,0:T(8,128)(2,1)S(1)}, u32[]{:S(2)}, u32[]{:S(2)}) %all-to-all-start.8) | async-done | bytes 147488 | tf_op jit(solution)/shard_map/all_to_all | solution.py:478
  462.3 6.1 %collective-permute-done.22 = bf16[768,768]{0,1:T(8,128)(2,1)} collective-permute-done((bf16[768,768]{0,1:T(8,128)(2,1)}, bf16[768,768]{0,1:T(8,128)(2,1)}, u32[]{:S(2)}, u32[]{:S(2)}) %collective-permute-start.22) | collective-permute-done | bytes 1179680 | tf_op jit(solution)/shard_map/ppermute | solution.py:493
  471.1 5.5 %collective-permute-start.23 = (bf16[768,768]{0,1:T(8,128)(2,1)}, bf16[768,768]{0,1:T(8,128)(2,1)}, u32[]{:S(2)}, u32[]{:S(2)}) collective-permute-start(bf16[768,768]{0,1:T(8,128)(2,1)} %fusion.23), channel_id=1, source_target_pairs={{0,1},{1,2},{2,3},{4,5},{5,6},{6,7},{8,9},{9,10},{10,11},{12,13},{... | collective-permute-start | bytes 3538952 | tf_op jit(solution)/shard_map/ppermute | solution.py:493
  478.9 6.6 %all-to-all-start.12 = ((bf16[4,96,768]{2,1,0:T(8,128)(2,1)}), bf16[4,96,768]{2,1,0:T(8,128)(2,1)}, u32[]{:S(2)}, u32[]{:S(2)}) async-start(bf16[4,96,768]{2,1,0:T(8,128)(2,1)} %add_convert_fusion.7), calls=%async_computation.12 | async-start | bytes 1179648 | tf_op jit(solution)/shard_map/all_to_all | solution.py:478
  502.0 10.1 %all-to-all-done.12 = bf16[4,96,768]{2,1,0:T(8,128)(2,1)} async-done(((bf16[4,96,768]{2,1,0:T(8,128)(2,1)}), bf16[4,96,768]{2,1,0:T(8,128)(2,1)}, u32[]{:S(2)}, u32[]{:S(2)}) %all-to-all-start.12) | async-done | bytes 589856 | tf_op jit(solution)/shard_map/all_to_all | solution.py:478
  (296 shorter events, 227.8 us)
Async XLA Ops:
  37.2 31.0 %all-to-all-start.4 = ((bf16[4,96,768]{2,1,0:T(8,128)(2,1)}), bf16[4,96,768]{2,1,0:T(8,128)(2,1)}, u32[]{:S(2)}, u32[]{:S(2)}) async-start(bf16[4,96,768]{2,1,0:T(8,128)(2,1)} %broadcast_in_dim.38), calls=%async_computation.4 | async-start | bytes 1179648 | tf_op jit(solution)/shard_map/all_to_all | solution.py:478
  68.2 30.3 %all-to-all-start = ((bf16[4,192,768]{2,1,0:T(8,128)(2,1)}), bf16[4,192,768]{2,1,0:T(8,128)(2,1)S(1)}, u32[]{:S(2)}, u32[]{:S(2)}) async-start(bf16[4,192,768]{2,1,0:T(8,128)(2,1)} %get-tuple-element.20), calls=%async_computation | async-start | bytes 2359296 | tf_op jit(solution)/shard_map/all_to_all | solution.py:556
  99.7 50.0 %all-to-all-start.1 = ((bf16[4,192,768]{2,1,0:T(8,128)(2,1)}), bf16[4,192,768]{2,1,0:T(8,128)(2,1)}, u32[]{:S(2)}, u32[]{:S(2)}) async-start(bf16[4,192,768]{2,1,0:T(8,128)(2,1)} %broadcast_in_dim.35), calls=%async_computation.1 | async-start | bytes 2359296 | tf_op jit(solution)/shard_map/all_to_all | solution.py:478
  111.0 26.7 %collective-permute-start = (bf16[4,96,768]{2,1,0:T(8,128)(2,1)}, bf16[4,96,768]{2,1,0:T(8,128)(2,1)}, u32[]{:S(2)}, u32[]{:S(2)}) collective-permute-start(bf16[4,96,768]{2,1,0:T(8,128)(2,1)} %all-to-all-done.2), channel_id=1, source_target_pairs={{0,8},{4,12},{8,0},{12,4},{16,24},{20,28},{24,16},{28,20},{1,9},{5... | collective-permute-start | bytes 1769480 | tf_op jit(solution)/shard_map/ppermute | solution.py:447
  115.0 26.4 %collective-permute-start.1 = (bf16[4,96,768]{2,1,0:T(8,128)(2,1)}, bf16[4,96,768]{2,1,0:T(8,128)(2,1)}, u32[]{:S(2)}, u32[]{:S(2)}) collective-permute-start(bf16[4,96,768]{2,1,0:T(8,128)(2,1)} %all-to-all-done.2), channel_id=1, source_target_pairs={{0,16},{4,20},{8,24},{12,28},{16,0},{20,4},{24,8},{28,12},{1,17},{... | collective-permute-start | bytes 1769480 | tf_op jit(solution)/shard_map/ppermute | solution.py:447
  133.8 25.6 %collective-permute-start.3 = (bf16[4,96,768]{2,1,0:T(8,128)(2,1)}, bf16[4,96,768]{2,1,0:T(8,128)(2,1)}, u32[]{:S(2)}, u32[]{:S(2)}) collective-permute-start(bf16[4,96,768]{2,1,0:T(8,128)(2,1)} %all-to-all-done.2), channel_id=1, source_target_pairs={{0,4},{4,0},{8,12},{12,8},{16,20},{20,16},{24,28},{28,24},{1,5},{5... | collective-permute-start | bytes 1769480 | tf_op jit(solution)/shard_map/ppermute | solution.py:447
  166.2 32.5 %collective-permute-start.20 = (bf16[4,96,768]{2,1,0:T(8,128)(2,1)}, bf16[4,96,768]{2,1,0:T(8,128)(2,1)S(1)}, u32[]{:S(2)}, u32[]{:S(2)}) collective-permute-start(bf16[4,96,768]{2,1,0:T(8,128)(2,1)} %collective-permute-done.16), channel_id=1, source_target_pairs={{0,4},{4,0},{8,12},{12,8},{16,20},{20,16},{24,28},{28,24},{1,5},{5... | collective-permute-start | bytes 1769480 | tf_op jit(solution)/shard_map/ppermute | solution.py:447
  266.7 30.9 %all-to-all-start.5 = ((bf16[4,192,768]{2,1,0:T(8,128)(2,1)}), bf16[4,192,768]{2,1,0:T(8,128)(2,1)}, u32[]{:S(2)}, u32[]{:S(2)}) async-start(bf16[4,192,768]{2,1,0:T(8,128)(2,1)} %bitcast.106), calls=%async_computation.5 | async-start | bytes 2359296 | tf_op jit(solution)/shard_map/all_to_all | solution.py:591
  277.8 103.4 %collective-permute-start.27 = (bf16[1536,768]{1,0:T(8,128)(2,1)}, bf16[1536,768]{1,0:T(8,128)(2,1)}, u32[]{:S(2)}, u32[]{:S(2)}) collective-permute-start(bf16[1536,768]{1,0:T(8,128)(2,1)} %convolution_convert_fusion.2), channel_id=1, source_target_pairs={{0,4},{4,0},{8,12},{12,8},{16,20},{20,16},{24,28},{28,24},{1,5},{5... | collective-permute-start | bytes 7077896 | tf_op jit(solution)/shard_map/ppermute | solution.py:447
  283.0 106.6 %collective-permute-start.31 = (bf16[1536,768]{1,0:T(8,128)(2,1)}, bf16[1536,768]{1,0:T(8,128)(2,1)}, u32[]{:S(2)}, u32[]{:S(2)}) collective-permute-start(bf16[1536,768]{1,0:T(8,128)(2,1)} %convolution_convert_fusion.1), channel_id=1, source_target_pairs={{0,4},{4,0},{8,12},{12,8},{16,20},{20,16},{24,28},{28,24},{1,5},{5... | collective-permute-start | bytes 7077896 | tf_op jit(solution)/shard_map/ppermute | solution.py:447
  297.6 105.8 %all-to-all-start.11 = ((f32[4,1,242]{2,1,0:T(1,128)}), f32[4,1,242]{2,1,0:T(1,128)S(1)}, u32[]{:S(2)}, u32[]{:S(2)}) async-start(f32[4,1,242]{2,1,0:T(1,128)} %all_to_all.57), calls=%async_computation.11 | async-start | bytes 8192 | tf_op jit(solution)/shard_map/all_to_all | solution.py:478
  355.2 43.8 %collective-permute-start.24 = (bf16[768,768]{0,1:T(8,128)(2,1)}, bf16[768,768]{0,1:T(8,128)(2,1)}, u32[]{:S(2)}, u32[]{:S(2)}) collective-permute-start(bf16[768,768]{0,1:T(8,128)(2,1)} %bitcast.105), channel_id=1, source_target_pairs={{3,2},{7,6},{11,10},{15,14},{19,18},{23,22},{27,26},{31,30}} | collective-permute-start | bytes 3538952 | tf_op jit(solution)/shard_map/ppermute | solution.py:494
  360.0 75.7 %collective-permute-start.21 = (bf16[768,768]{0,1:T(8,128)(2,1)}, bf16[768,768]{0,1:T(8,128)(2,1)}, u32[]{:S(2)}, u32[]{:S(2)}) collective-permute-start(bf16[768,768]{0,1:T(8,128)(2,1)} %bitcast.104), channel_id=1, source_target_pairs={{0,1},{4,5},{8,9},{12,13},{16,17},{20,21},{24,25},{28,29}} | collective-permute-start | bytes 3538952 | tf_op jit(solution)/shard_map/ppermute | solution.py:493
  388.8 61.3 %collective-permute-start.28 = (bf16[4,96,768]{2,1,0:T(8,128)(2,1)}, bf16[4,96,768]{2,1,0:T(8,128)(2,1)}, u32[]{:S(2)}, u32[]{:S(2)}) collective-permute-start(bf16[4,96,768]{2,1,0:T(8,128)(2,1)} %bitcast.28), channel_id=1, source_target_pairs={{0,16},{4,20},{8,24},{12,28},{16,0},{20,4},{24,8},{28,12},{1,17},{... | collective-permute-start | bytes 1769480 | tf_op jit(solution)/shard_map/ppermute | solution.py:447
  395.5 50.5 %collective-permute-start.33 = (bf16[4,96,768]{2,1,0:T(8,128)(2,1)}, bf16[4,96,768]{2,1,0:T(8,128)(2,1)}, u32[]{:S(2)}, u32[]{:S(2)}) collective-permute-start(bf16[4,96,768]{2,1,0:T(8,128)(2,1)} %bitcast.41), channel_id=1, source_target_pairs={{0,8},{4,12},{8,0},{12,4},{16,24},{20,28},{24,16},{28,20},{1,9},{5... | collective-permute-start | bytes 1769480 | tf_op jit(solution)/shard_map/ppermute | solution.py:447
  401.6 56.6 %collective-permute-start.25 = (bf16[768,768]{0,1:T(8,128)(2,1)}, bf16[768,768]{0,1:T(8,128)(2,1)}, u32[]{:S(2)}, u32[]{:S(2)}) collective-permute-start(bf16[768,768]{0,1:T(8,128)(2,1)} %fusion.20), channel_id=1, source_target_pairs={{3,2},{2,1},{7,6},{6,5},{11,10},{10,9},{15,14},{14,13},{19,18},{18... | collective-permute-start | bytes 3538952 | tf_op jit(solution)/shard_map/ppermute | solution.py:494
  403.3 28.1 %all-to-all-start.8 = ((bf16[4,96,192]{2,1,0:T(8,128)(2,1)}), bf16[4,96,192]{2,1,0:T(8,128)(2,1)S(1)}, u32[]{:S(2)}, u32[]{:S(2)}) async-start(bf16[4,96,192]{2,1,0:T(8,128)(2,1)} %copy.143), calls=%async_computation.8 | async-start | bytes 393216 | tf_op jit(solution)/shard_map/all_to_all | solution.py:478
  409.8 41.8 %collective-permute-start.30 = (bf16[4,96,768]{2,1,0:T(8,128)(2,1)}, bf16[4,96,768]{2,1,0:T(8,128)(2,1)}, u32[]{:S(2)}, u32[]{:S(2)}) collective-permute-start(bf16[4,96,768]{2,1,0:T(8,128)(2,1)} %fusion.31), channel_id=1, source_target_pairs={{0,8},{4,12},{8,0},{12,4},{16,24},{20,28},{24,16},{28,20},{1,9},{5... | collective-permute-start | bytes 1769480 | tf_op jit(solution)/shard_map/ppermute | solution.py:447
  438.3 30.2 %collective-permute-start.22 = (bf16[768,768]{0,1:T(8,128)(2,1)}, bf16[768,768]{0,1:T(8,128)(2,1)}, u32[]{:S(2)}, u32[]{:S(2)}) collective-permute-start(bf16[768,768]{0,1:T(8,128)(2,1)} %fusion.22), channel_id=1, source_target_pairs={{0,1},{1,2},{4,5},{5,6},{8,9},{9,10},{12,13},{13,14},{16,17},{17,1... | collective-permute-start | bytes 3538952 | tf_op jit(solution)/shard_map/ppermute | solution.py:493
  446.0 30.6 %collective-permute-start.32 = (bf16[4,96,768]{2,1,0:T(8,128)(2,1)}, bf16[4,96,768]{2,1,0:T(8,128)(2,1)}, u32[]{:S(2)}, u32[]{:S(2)}) collective-permute-start(bf16[4,96,768]{2,1,0:T(8,128)(2,1)} %bitcast.110), channel_id=1, source_target_pairs={{0,8},{4,12},{8,0},{12,4},{16,24},{20,28},{24,16},{28,20},{1,9},{5... | collective-permute-start | bytes 1769480 | tf_op jit(solution)/shard_map/ppermute | solution.py:447
  450.2 26.4 %collective-permute-start.34 = (bf16[4,96,768]{2,1,0:T(8,128)(2,1)}, bf16[4,96,768]{2,1,0:T(8,128)(2,1)}, u32[]{:S(2)}, u32[]{:S(2)}) collective-permute-start(bf16[4,96,768]{2,1,0:T(8,128)(2,1)} %fusion.29), channel_id=1, source_target_pairs={{0,16},{4,20},{8,24},{12,28},{16,0},{20,4},{24,8},{28,12},{1,17},{... | collective-permute-start | bytes 1769480 | tf_op jit(solution)/shard_map/ppermute | solution.py:447
  460.9 53.2 %collective-permute-start.26 = (bf16[768,768]{0,1:T(8,128)(2,1)}, bf16[768,768]{0,1:T(8,128)(2,1)}, u32[]{:S(2)}, u32[]{:S(2)}) collective-permute-start(bf16[768,768]{0,1:T(8,128)(2,1)} %fusion.21), channel_id=1, source_target_pairs={{3,2},{2,1},{1,0},{7,6},{6,5},{5,4},{11,10},{10,9},{9,8},{15,14},{... | collective-permute-start | bytes 3538952 | tf_op jit(solution)/shard_map/ppermute | solution.py:494
  471.1 43.0 %collective-permute-start.23 = (bf16[768,768]{0,1:T(8,128)(2,1)}, bf16[768,768]{0,1:T(8,128)(2,1)}, u32[]{:S(2)}, u32[]{:S(2)}) collective-permute-start(bf16[768,768]{0,1:T(8,128)(2,1)} %fusion.23), channel_id=1, source_target_pairs={{0,1},{1,2},{2,3},{4,5},{5,6},{6,7},{8,9},{9,10},{10,11},{12,13},{... | collective-permute-start | bytes 3538952 | tf_op jit(solution)/shard_map/ppermute | solution.py:493
  478.9 33.3 %all-to-all-start.12 = ((bf16[4,96,768]{2,1,0:T(8,128)(2,1)}), bf16[4,96,768]{2,1,0:T(8,128)(2,1)}, u32[]{:S(2)}, u32[]{:S(2)}) async-start(bf16[4,96,768]{2,1,0:T(8,128)(2,1)} %add_convert_fusion.7), calls=%async_computation.12 | async-start | bytes 1179648 | tf_op jit(solution)/shard_map/all_to_all | solution.py:478
  (59 other events, 758.5 us)
